TPU v7x, 32 devices: a 4x4x1 block of a 4x4x8 slice. The times are simulated.
32 devices in a mesh: dp: 1 (over z), tp: 4 (over y), wg: 8 (over x, core).
Axes of the slice: x: 4, y: 4, z: 1, core: 2. Of those that a mesh axis runs over, the one named last changes fastest.
The devices are a block of a 4x4x8 slice.
Arguments:
- x_in: bfloat16 [16, 2048, 2048], P(('dp', 'wg'))
- valid: int32 [16, 2048], P(('dp', 'wg'))
- ln_gain: float32 [2048], replicated
- w_q: bfloat16 [2048, 2048], P('wg', 'tp')
- w_kv: bfloat16 [2048, 512], P('wg')
- w_gate: bfloat16 [2048, 16384], P('wg', 'tp')
- w_up: bfloat16 [2048, 16384], P('wg', 'tp')
- w_o: bfloat16 [2048, 2048], P('tp', 'wg')
- w_down: bfloat16 [16384, 2048], P('tp', 'wg')
Outputs:
- output 1: bfloat16 [16, 2048, 2048], P(('dp', 'wg'))
- output 2: bfloat16 [16, 2048, 256], P(('dp', 'wg'))
- output 3: bfloat16 [16, 2048, 256], P(('dp', 'wg'))
All inputs are finite; a program needn't handle non-finite values.
Results may differ from a plain program's by a relative error of at most 0.0137817.
Values are sent between devices in bfloat16 or wider.
A program may use at most 768 MiB of HBM per device.

v0:
```python
import jax
import jax.numpy as jnp
from jax import lax
from jax.sharding import PartitionSpec as P, NamedSharding


def layer_norm(x_in, ln_gain):
    x_f32 = x_in.astype(jnp.float32)
    mean = x_f32.mean(axis=-1, keepdims=True)
    centered = x_f32 - mean
    x_var = (centered * centered).mean(axis=-1, keepdims=True)
    return (centered * lax.rsqrt(x_var + 1e-6) * ln_gain).astype(jnp.bfloat16)


def rope_tables(seq_len, head_dim):
    half = head_dim // 2
    inv_freq = 10000.0 ** (-2.0 * jnp.arange(half, dtype=jnp.float32) / head_dim)
    angles = jnp.arange(seq_len, dtype=jnp.float32)[:, None] * inv_freq[None, :]
    return jnp.cos(angles), jnp.sin(angles)


def apply_rope(vals, cos_t, sin_t):
    half = vals.shape[-1] // 2
    first = vals[..., :half]
    second = vals[..., half:]
    return jnp.concatenate([first * cos_t - second * sin_t, second * cos_t + first * sin_t], axis=-1)


def attend_and_mix(q_proj, kv_proj, gate_proj, up_proj, valid):
    batch, seq_len, q_cols = q_proj.shape
    head_dim = kv_proj.shape[-1] // 2
    n_heads = q_cols // head_dim
    cos_t, sin_t = rope_tables(seq_len, head_dim)
    q_heads = q_proj.reshape(batch, seq_len, n_heads, head_dim).astype(jnp.float32)
    q_rot = apply_rope(q_heads, cos_t[None, :, None, :], sin_t[None, :, None, :]).astype(jnp.bfloat16)
    k_rot = apply_rope(kv_proj[..., :head_dim].astype(jnp.float32), cos_t[None], sin_t[None]).astype(jnp.bfloat16)
    v_rows = kv_proj[..., head_dim:]
    scores = jnp.einsum('bshe,bte->bhst', q_rot, k_rot, preferred_element_type=jnp.float32) * head_dim ** -0.5
    positions = jnp.arange(seq_len)
    allowed = (positions[None, :] <= positions[:, None])[None, None] & (valid[:, None, None, :] > 0)
    scores = jnp.where(allowed, scores, -1e30)
    probs = jax.nn.softmax(scores, axis=-1).astype(jnp.bfloat16)
    attn_out = jnp.einsum('bhst,bte->bshe', probs, v_rows, preferred_element_type=jnp.float32).astype(jnp.bfloat16)
    mlp_out = (jax.nn.silu(gate_proj.astype(jnp.float32)) * up_proj.astype(jnp.float32)).astype(jnp.bfloat16)
    return attn_out.reshape(batch, seq_len, q_cols), mlp_out, k_rot, v_rows


def solution(mesh):
    batch_spec = P(('dp', 'wg'), None, None)
    in_specs = (batch_spec, P(('dp', 'wg'), None), P(None), P('wg', 'tp'), P('wg', None),
                P('wg', 'tp'), P('wg', 'tp'), P('tp', 'wg'), P('tp', 'wg'))
    out_specs = (batch_spec, batch_spec, batch_spec)

    def local_step(x_in, valid, ln_gain, w_q, w_kv, w_gate, w_up, w_o, w_down):
        wq_full = lax.all_gather(w_q, 'wg', axis=0, tiled=True)
        wkv_full = lax.all_gather(w_kv, 'wg', axis=0, tiled=True)
        wgate_full = lax.all_gather(w_gate, 'wg', axis=0, tiled=True)
        wup_full = lax.all_gather(w_up, 'wg', axis=0, tiled=True)
        wo_full = lax.all_gather(w_o, 'wg', axis=1, tiled=True)
        wdown_full = lax.all_gather(w_down, 'wg', axis=1, tiled=True)
        normed = layer_norm(x_in, ln_gain)
        q_proj = jnp.einsum('bsd,dk->bsk', normed, wq_full, preferred_element_type=jnp.float32).astype(jnp.bfloat16)
        kv_proj = jnp.einsum('bsd,dk->bsk', normed, wkv_full, preferred_element_type=jnp.float32).astype(jnp.bfloat16)
        gate_proj = jnp.einsum('bsd,dk->bsk', normed, wgate_full, preferred_element_type=jnp.float32).astype(jnp.bfloat16)
        up_proj = jnp.einsum('bsd,dk->bsk', normed, wup_full, preferred_element_type=jnp.float32).astype(jnp.bfloat16)
        attn_flat, mlp_out, k_rot, v_rows = attend_and_mix(q_proj, kv_proj, gate_proj, up_proj, valid)
        part_out = (jnp.einsum('bsk,kd->bsd', attn_flat, wo_full, preferred_element_type=jnp.float32)
                    + jnp.einsum('bsk,kd->bsd', mlp_out, wdown_full, preferred_element_type=jnp.float32)).astype(jnp.bfloat16)
        total = lax.psum(part_out, 'tp')
        y_out = (x_in.astype(jnp.float32) + total.astype(jnp.float32)).astype(jnp.bfloat16)
        keep = valid[..., None] > 0
        return y_out, jnp.where(keep, k_rot, 0), jnp.where(keep, v_rows, 0)

    return jax.shard_map(local_step, mesh=mesh, in_specs=in_specs, out_specs=out_specs, check_vma=False)
```

profile of v0, /device:TPU:97, one launch (start us, length us, event | category | flops | bytes accessed | tf_op | source)
XLA Modules:
  0.0 759.7 jit_solution(15682174401828614652)
XLA Ops:
  9.2 1.8 copy.12
  13.8 4.1 iota_compare_fusion
  18.0 7.5 convert_reduce_fusion
  25.5 3.5 copy-done
  29.0 5.5 fusion.9
  34.5 3.7 fusion.53
  39.9 7.3 broadcast_and_fusion
  47.2 13.7 %convolution_convert_fusion = bf16[2,2048,512]{1,2,0:T(8,128)(2,1)S(1)} fusion(bf16[2048,512]{0,1:T(8,128)(2,1)} %all-gather.9.cloned.1.call-done, bf16[2,2048,2048]{2,1,0:T(8,128)(2,1)} %param.9, f32[2048]{0:T(1024)S(1)} %copy-done.16, f32[2,2048]{1,0:T(2,128)S(1)} %add_rsqrt_fusion, f32[2,2048]{1,0:T(2,128)S(1)} %broadcast_multiply_fusion), kind=kOutput, calls=%fused_computation.39 | convolution fusion | flops 8633974784 | bytes 23109632 | tf_op jit(solution)/shard_map/bsd,dk->bsk/dot_general | solution.py:62
  60.9 4.3 fusion.74
  65.2 5.4 copy.30
  70.6 5.4 copy.29
  76.0 14.0 %convolution_convert_fusion.1 = bf16[2,2048,512]{1,2,0:T(8,128)(2,1)S(1)} fusion(bf16[2048,512]{0,1:T(8,128)(2,1)} %all-gather.7.cloned.1.call-done, bf16[2,2048,2048]{2,1,0:T(8,128)(2,1)} %param.9, f32[2048]{0:T(1024)S(1)} %copy-done.16, f32[2,2048]{1,0:T(2,128)S(1)} %add_rsqrt_fusion, f32[2,2048]{1,0:T(2,128)S(1)} %broadcast_multiply_fusion), kind=kOutput, calls=%fused_computation.40 | convolution fusion | flops 8633974784 | bytes 23109632 | tf_op jit(solution)/shard_map/bsd,dk->bsk/dot_general | solution.py:63
  91.8 2.1 subtract_convert_fusion.1
  96.6 3.1 subtract_convert_fusion
  99.7 30.3 %fusion.75 = f32[2,2,2048]{2,1,0:T(2,128)S(1)} fusion(pred[2,2048,2048]{1,2,0:T(8,128)(4,1)} %broadcast_and_fusion, bf16[2,2048,2,128]{3,1,2,0:T(8,128)(2,1)} %get-tuple-element.7, bf16[2,2048,2,128]{3,1,2,0:T(8,128)(2,1)} %get-tuple-element.6, bf16[2,2048,128]{1,2,0:T(8,128)(2,1)S(1)} %copy-done.8, bf16[2,2048,128]{1,2,0:T(8,128)(2,1)S(1)} %copy-done.6), kind=kOutput, calls=%fused_computation.74 | convolution fusion | flops 8669628416 | bytes 14712832 | tf_op jit(solution)/shard_map/sub | solution.py:42
  130.1 37.0 %fusion.30 = bf16[2,256,2,2048]{3,1,2,0:T(8,128)(2,1)} fusion(f32[2,2,2048]{2,1,0:T(2,128)S(1)} %fusion.75, pred[2,2048,2048]{1,2,0:T(8,128)(4,1)} %broadcast_and_fusion, bf16[2,2048,512]{1,2,0:T(8,128)(2,1)} %copy-done.5, bf16[2,2048,2,128]{3,1,2,0:T(8,128)(2,1)} %get-tuple-element.7, bf16[2,2048,2,128]{3,1,2,0:T(8,128)(2,1)} %get-tuple-element.6, ...), kind=kOutput, calls=%fused_computation.38 | convolution fusion | flops 17278445568 | bytes 21004288 | tf_op jit(solution)/shard_map/bhst,bte->bshe/dot_general | solution.py:43
  167.1 18.3 %fusion.47 = f32[2,2048,2048]{2,1,0:T(8,128)} fusion(bf16[2,2048,512]{1,2,0:T(8,128)(2,1)} %bitcast.88, bf16[512,2048]{1,0:T(8,128)(2,1)} %all-gather.11.cloned.1.call-done), kind=kOutput, calls=%fused_computation.48 | convolution fusion | flops 8589934592 | bytes 39845888 | tf_op jit(solution)/shard_map/bsk,kd->bsd/dot_general | solution.py:67
  185.4 83.7 %fusion.22 = bf16[2,2048,4096]{2,1,0:T(8,128)(2,1)} fusion(bf16[2048,4096]{1,0:T(8,128)(2,1)} %all-gather.13.cloned.1.call-done, bf16[2,2048,2048]{2,1,0:T(8,128)(2,1)} %param.9, f32[2048]{0:T(1024)S(1)} %copy-done.17, f32[2,2048]{1,0:T(2,128)S(1)} %copy-done.15, f32[2,2048]{1,0:T(2,128)S(1)} %copy-done.12), kind=kOutput, calls=%fused_computation.30 | convolution fusion | flops 68761419776 | bytes 67149824 | tf_op jit(solution)/shard_map/bsd,dk->bsk/dot_general | solution.py:64
  269.1 83.4 %fusion.20 = bf16[2,2048,4096]{2,1,0:T(8,128)(2,1)} fusion(bf16[2048,4096]{1,0:T(8,128)(2,1)} %all-gather.15.cloned.1.call-done, bf16[2,2048,2048]{2,1,0:T(8,128)(2,1)} %param.9, f32[2048]{0:T(1024)S(1)} %copy-done.17, f32[2,2048]{1,0:T(2,128)S(1)} %copy-done.15, f32[2,2048]{1,0:T(2,128)S(1)} %copy-done.12), kind=kOutput, calls=%fused_computation.28 | convolution fusion | flops 68761419776 | bytes 67149824 | tf_op jit(solution)/shard_map/bsd,dk->bsk/dot_general | solution.py:65
  352.5 86.9 %add_convert_fusion = bf16[2,2048,2048]{2,1,0:T(8,128)(2,1)} fusion(f32[2,2048,2048]{2,1,0:T(8,128)} %fusion.47, bf16[4096,2048]{1,0:T(8,128)(2,1)} %all-gather.17.cloned.1.call-done, bf16[2,2048,4096]{2,1,0:T(8,128)(2,1)} %fusion.20, bf16[2,2048,4096]{2,1,0:T(8,128)(2,1)} %fusion.22), kind=kOutput, calls=%fused_computation.21 | convolution fusion | flops 68870471680 | bytes 134217728 | tf_op jit(solution)/shard_map/bsk,kd->bsd/dot_general | solution.py:68
  441.0 2.5 copy.22
  445.1 2.5 copy.21
  447.6 285.1 %all-reduce.2.cloned.1.call-done = bf16[2,2048,2048]{2,1,0:T(8,128)(2,1)} async-done(((bf16[2,2048,2048]{2,1,0:T(8,128)(2,1)}), bf16[2,2048,2048]{2,1,0:T(8,128)(2,1)}) %all-reduce.2.cloned.1.call-update) | async-done | bytes 16777232 | tf_op jit(solution)/shard_map/psum | solution.py:69
  732.7 19.9 %fusion.12 = bf16[2,2048,2048]{2,1,0:T(8,128)(2,1)} fusion(bf16[2,2048,2048]{2,1,0:T(8,128)(2,1)} %param.9, bf16[2,2048,2048]{2,1,0:T(8,128)(2,1)} %all-reduce.2.cloned.1.call-done), kind=kLoop, calls=%fused_computation.20 | loop fusion | flops 33554432 | bytes 50331648 | tf_op jit(solution)/shard_map/convert_element_type | solution.py:70
  (64 shorter events, 14.2 us)
Async XLA Ops:
  7.2 10.8 %copy-start.13 = (s32[2,2048]{1,0:T(2,128)S(1)}, s32[2,2048]{1,0:T(2,128)}, u32[]{:S(2)}) copy-start(s32[2,2048]{1,0:T(2,128)} %param.10) | copy-start | bytes 49156
  7.2 40.0 %all-gather.9.cloned.1.call-start = ((), (), s32[]{:S(2)}) async-start(), calls=%async_computation.1 | async-start | bytes 2359296 | tf_op jit(solution)/shard_map/all_gather | solution.py:55
  9.1 66.9 %all-gather.7.cloned.1.call-start = ((), (), s32[]{:S(2)}) async-start(), calls=%async_computation | async-start | bytes 2359296 | tf_op jit(solution)/shard_map/all_gather | solution.py:56
  11.0 156.1 %all-gather.11.cloned.1.call-start = ((), (), s32[]{:S(2)}) async-start(), calls=%async_computation.2 | async-start | bytes 2359296 | tf_op jit(solution)/shard_map/all_gather | solution.py:59
  11.8 173.6 %all-gather.13.cloned.1.call-start = ((), (), s32[]{:S(2)}) async-start(), calls=%async_computation.3 | async-start | bytes 18874368 | tf_op jit(solution)/shard_map/all_gather | solution.py:57
  12.5 256.6 %all-gather.15.cloned.1.call-start = ((), (), s32[]{:S(2)}) async-start(), calls=%async_computation.4 | async-start | bytes 18874368 | tf_op jit(solution)/shard_map/all_gather | solution.py:58
  13.1 339.4 %all-gather.17.cloned.1.call-start = ((), (), s32[]{:S(2)}) async-start(), calls=%async_computation.5 | async-start | bytes 18874368 | tf_op jit(solution)/shard_map/all_gather | solution.py:60
  13.8 719.0 %all-reduce.2.cloned.1.call-start = ((), (), s32[]{:S(2)}) async-start(), calls=%async_computation.6 | async-start | bytes 33554432 | tf_op jit(solution)/shard_map/psum | solution.py:69
  18.0 72.0 %copy-start.9 = (pred[2,2048]{1,0:T(4,128)(4,1)}, pred[2,2048]{1,0:T(4,128)(4,1)S(1)}, u32[]{:S(2)}) copy-start(pred[2,2048]{1,0:T(4,128)(4,1)S(1)} %broadcast_compare_fusion) | copy-start | bytes 12292
  18.0 11.0 %copy-start = (bf16[2,2048,2048]{2,1,0:T(8,128)(2,1)S(1)}, bf16[2,2048,2048]{2,1,0:T(8,128)(2,1)}, u32[]{:S(2)}) copy-start(bf16[2,2048,2048]{2,1,0:T(8,128)(2,1)} %param.9) | copy-start | bytes 50331652
  29.0 46.9 %copy-start.11 = (f32[2,2048]{1,0:T(2,128)}, f32[2,2048]{1,0:T(2,128)S(1)}, u32[]{:S(2)}) copy-start(f32[2,2048]{1,0:T(2,128)S(1)} %broadcast_multiply_fusion) | copy-start | bytes 49156
  34.5 41.5 %copy-start.14 = (f32[2,2048]{1,0:T(2,128)}, f32[2,2048]{1,0:T(2,128)S(1)}, u32[]{:S(2)}) copy-start(f32[2,2048]{1,0:T(2,128)S(1)} %add_rsqrt_fusion) | copy-start | bytes 49156
  38.2 9.0 %copy-start.16 = (f32[2048]{0:T(1024)S(1)}, f32[2048]{0:T(1024)}, u32[]{:S(2)}) copy-start(f32[2048]{0:T(1024)} %param.11) | copy-start | bytes 24580
  90.0 4.2 copy-start.5
  90.0 5.2 copy-start.1
  90.0 6.4 copy-start.2
  90.0 6.6 copy-start.4
  96.6 3.1 copy-start.6
  96.6 3.1 copy-start.8
  167.1 18.3 %copy-start.12 = (f32[2,2048]{1,0:T(2,128)S(1)}, f32[2,2048]{1,0:T(2,128)}, u32[]{:S(2)}) copy-start(f32[2,2048]{1,0:T(2,128)} %copy-done.11) | copy-start | bytes 49156
  167.1 18.3 %copy-start.15 = (f32[2,2048]{1,0:T(2,128)S(1)}, f32[2,2048]{1,0:T(2,128)}, u32[]{:S(2)}) copy-start(f32[2,2048]{1,0:T(2,128)} %copy-done.14) | copy-start | bytes 49156
  167.1 18.3 %copy-start.17 = (f32[2048]{0:T(1024)S(1)}, f32[2048]{0:T(1024)}, u32[]{:S(2)}) copy-start(f32[2048]{0:T(1024)} %param.11) | copy-start | bytes 24580
  439.4 4.1 copy-start.7
  439.4 4.1 copy-start.10
  (1 other events, 1.6 us)
Sparse Core Ops, SparseCore 0:
  10.2 28.5 all-gather.8
  40.4 25.1 all-gather.6
  67.1 25.1 all-gather.10
  93.8 83.2 all-gather.12
  178.6 82.9 all-gather.14
  263.0 87.8 all-gather.16
  439.6 293.1 all-reduce.1
where the time goes:
time: 763 us; the launch traced here: 760 us
  matrix products  367 us (48%)
  waiting for transfers between devices  288 us (38%)
  other arithmetic  56.6 us (7%)
  local copies, waits for them, and re-layouts  33.1 us (4%)
  between operations  14.6 us (2%)
    psum x1, waiting for transfers between devices, local_step(): total = lax.psum(part_out, 'tp')  285 us
    dot_general x1, matrix products, local_step(): jnp.einsum('bsk,kd->bsd', mlp_out, wdown_full, preferred_element_type=jnp...  86.9 us
    dot_general x1, matrix products, local_step(): jnp.einsum('bsd,dk->bsk', normed, wgate_full, preferred_element_type=jnp....  83.7 us
    dot_general x1, matrix products, local_step(): jnp.einsum('bsd,dk->bsk', normed, wup_full, preferred_element_type=jnp.fl...  83.4 us
    dot_general x1, matrix products, attend_and_mix(): jnp.einsum('bhst,bte->bshe', probs, v_rows, preferred_element_type=jnp.fl...  37 us
    sub x1, matrix products, attend_and_mix(): probs = jax.nn.softmax(scores, axis=-1).astype(jnp.bfloat16)  30.3 us
    unnamed x42, local copies, waits for them, and re-layouts  27.2 us
    convert_element_type x1, other arithmetic, local_step(): (x_in.astype(jnp.float32) + total.astype(jnp.float32)).astype(jnp.bfloat16)  19.9 us
  transfers between devices with their start and end apart: 7, of which 1 were waited for; matrix products, arithmetic and copies ran while one was open for 45% of the time, Pallas kernels for 0%

commit v1 on v0

v1 whole, which is shorter than its diff:
```python
import functools

import jax
import jax.numpy as jnp
from jax import lax
from jax.experimental import pallas as pl
from jax.experimental.pallas import tpu as pltpu
from jax.sharding import PartitionSpec as P


F32 = jnp.float32
BF16 = jnp.bfloat16
N_PIECES = 8
FF_TILE = 512
VMEM_LIMIT = 60 * 1024 * 1024


def after(val, *deps):
    return lax.optimization_barrier((val,) + deps)[0]


def params(sem):
    return pltpu.CompilerParams(dimension_semantics=sem, vmem_limit_bytes=VMEM_LIMIT)


def cost(flops, nbytes):
    return pl.CostEstimate(flops=int(flops), bytes_accessed=int(nbytes), transcendentals=0)


def ln_kernel(pos_ref, x_ref, gain_ref, z_ref):
    sub = 32
    blk = x_ref.shape[1] // N_PIECES

    def body(i, carry):
        rows = pl.ds(pl.multiple_of(i * sub, sub), sub)
        x = x_ref[rows, :].astype(F32)
        mean = jnp.mean(x, axis=-1, keepdims=True)
        cen = x - mean
        var = jnp.mean(cen * cen, axis=-1, keepdims=True)
        z = (cen * lax.rsqrt(var + 1e-6) * gain_ref[...]).astype(BF16)
        for j in range(N_PIECES):
            z_ref[rows, pl.ds(pl.multiple_of(pos_ref[j] * blk, blk), blk)] = z[:, j * blk:(j + 1) * blk]
        return carry

    lax.fori_loop(0, x_ref.shape[0] // sub, body, 0, unroll=2)


def layer_norm(x, gain, pos, prompt, seq):
    dim = x.shape[1]
    tm = 512
    n_m = seq // tm
    return pl.pallas_call(
        ln_kernel,
        grid_spec=pltpu.PrefetchScalarGridSpec(
            num_scalar_prefetch=1, grid=(n_m,),
            in_specs=[pl.BlockSpec((tm, dim), lambda i, p: (prompt * n_m + i, 0)),
                      pl.BlockSpec((1, dim), lambda i, p: (0, 0))],
            out_specs=pl.BlockSpec((tm, dim), lambda i, p: (i, 0))),
        out_shape=jax.ShapeDtypeStruct((seq, dim), BF16),
        compiler_params=params(("arbitrary",)),
        cost_estimate=cost(5e9, seq * dim * 4),
        name="ln",
    )(pos, x, gain.reshape(1, dim))


def fill_rows(w_s, pieces, col=0):
    row = 0
    for p in pieces:
        w_s[pl.ds(row, p.shape[0]), pl.ds(col, p.shape[1])] = p[...]
        row += p.shape[0]


def apply_rope(vals, cos_t, sin_t):
    half = vals.shape[-1] // 2
    a, b = vals[:, :half], vals[:, half:]
    return a * cos_t - b * sin_t, b * cos_t + a * sin_t


def qkv_kernel(n_heads, hd, aliased, *refs):
    z_ref, cos_ref, sin_ref, valid_ref = refs[:4]
    pieces = refs[4:-5 - aliased]
    q_ref, k_ref, v_ref, vr_ref, w_s = refs[-5:]

    @pl.when(pl.program_id(0) == 0)
    def _():
        fill_rows(w_s, pieces)

    half = hd // 2
    sub = 256
    for r in range(0, z_ref.shape[0], sub):
        rows = pl.ds(r, sub)
        out = jnp.dot(z_ref[rows, :], w_s[...], preferred_element_type=F32).astype(BF16)
        cos_t, sin_t = cos_ref[rows, :], sin_ref[rows, :]
        keep = valid_ref[rows, :] > 0
        for h in range(n_heads):
            a, b = apply_rope(out[:, h * hd:(h + 1) * hd].astype(F32), cos_t, sin_t)
            q_ref[rows, h * hd:h * hd + half] = a.astype(BF16)
            q_ref[rows, h * hd + half:(h + 1) * hd] = b.astype(BF16)
        base = n_heads * hd
        a, b = apply_rope(out[:, base:base + hd].astype(F32), cos_t, sin_t)
        k_ref[rows, :half] = jnp.where(keep, a, 0.0).astype(BF16)
        k_ref[rows, half:] = jnp.where(keep, b, 0.0).astype(BF16)
        v = out[:, base + hd:]
        vr_ref[rows, :] = v
        v_ref[rows, :] = jnp.where(keep, v.astype(F32), 0.0).astype(BF16)


def qkv(z, pieces, cos_t, sin_t, valid_col, hd, prompt, caches):
    seq, dim = z.shape
    rows = valid_col.shape[0]
    cols = pieces[0].shape[1]
    n_heads = cols // hd - 2
    tm = 1024
    n_m = seq // tm
    full = lambda p: pl.BlockSpec(p.shape, lambda i: (0, 0))
    ops = [z, cos_t, sin_t, valid_col] + list(pieces) + list(caches)
    at = len(ops) - len(caches)
    cache_spec = pl.BlockSpec((tm, hd), lambda i: (prompt * n_m + i, 0))
    return pl.pallas_call(
        functools.partial(qkv_kernel, n_heads, hd, len(caches)),
        grid=(n_m,),
        in_specs=[pl.BlockSpec((tm, dim), lambda i: (i, 0)),
                  pl.BlockSpec((tm, hd // 2), lambda i: (i, 0)),
                  pl.BlockSpec((tm, hd // 2), lambda i: (i, 0)),
                  pl.BlockSpec((tm, 1), lambda i: (prompt * n_m + i, 0))] + [full(p) for p in pieces]
        + [pl.BlockSpec(memory_space=pl.ANY)] * len(caches),
        out_specs=[pl.BlockSpec((tm, n_heads * hd), lambda i: (i, 0)), cache_spec, cache_spec,
                   pl.BlockSpec((tm, hd), lambda i: (i, 0))],
        out_shape=[jax.ShapeDtypeStruct((seq, n_heads * hd), BF16)] + [jax.ShapeDtypeStruct((rows, hd), BF16)] * 2
        + [jax.ShapeDtypeStruct((seq, hd), BF16)],
        scratch_shapes=[pltpu.VMEM((dim, cols), BF16)],
        input_output_aliases={at + i: 1 + i for i in range(len(caches))},
        compiler_params=params(("arbitrary",)),
        cost_estimate=cost(2 * seq * dim * cols, seq * dim * 4),
        name="qkv",
    )(*ops)


def attn_kernel(n_blk, scale, q_ref, k_ref, v_ref, valid_ref, o_ref):
    i = pl.program_id(1)
    blk = q_ref.shape[0]
    dn = (((1,), (1,)), ((), ()))

    def block(b):
        past = b * blk
        q = q_ref[...]
        s1 = lax.dot_general(q, k_ref[past:past + blk, :], dn, preferred_element_type=F32) * scale
        rows = lax.broadcasted_iota(jnp.int32, (blk, blk), 0)
        cols = lax.broadcasted_iota(jnp.int32, (blk, blk), 1)
        ok1 = jnp.logical_and(cols <= rows, valid_ref[:, past:past + blk] > 0)
        s1 = jnp.where(ok1, s1, -1e30)
        top = jnp.max(s1, axis=-1, keepdims=True)
        if b:
            s0 = lax.dot_general(q, k_ref[:past, :], dn, preferred_element_type=F32) * scale
            s0 = jnp.where(valid_ref[:, :past] > 0, s0, -1e30)
            top = jnp.maximum(top, jnp.max(s0, axis=-1, keepdims=True))
            e0 = jnp.exp(s0 - top)
        e1 = jnp.exp(s1 - top)
        tot = jnp.sum(e1, axis=-1, keepdims=True)
        if b:
            tot = tot + jnp.sum(e0, axis=-1, keepdims=True)
        inv = 1.0 / tot
        out = jnp.dot((e1 * inv).astype(BF16), v_ref[past:past + blk, :], preferred_element_type=F32)
        if b:
            out = out + jnp.dot((e0 * inv).astype(BF16), v_ref[:past, :], preferred_element_type=F32)
        o_ref[...] = out.astype(BF16)

    for b in range(n_blk):
        pl.when(i == b)(functools.partial(block, b))


def attention(q, k, v, valid_row, prompt, act_cols):
    seq, hd = v.shape
    n_heads = q.shape[1] // hd
    blk = 512
    n_blk = seq // blk
    return pl.pallas_call(
        functools.partial(attn_kernel, n_blk, hd ** -0.5),
        grid=(n_heads, n_blk),
        in_specs=[pl.BlockSpec((blk, hd), lambda h, i: (i, h)),
                  pl.BlockSpec((seq, hd), lambda h, i: (prompt, 0)),
                  pl.BlockSpec((seq, hd), lambda h, i: (0, 0)),
                  pl.BlockSpec((None, 1, seq), lambda h, i: (prompt, 0, 0))],
        out_specs=pl.BlockSpec((blk, hd), lambda h, i: (i, h)),
        out_shape=jax.ShapeDtypeStruct((seq, act_cols), BF16),
        compiler_params=params(("arbitrary", "arbitrary")),
        cost_estimate=cost(16e9, seq * hd * 12),
        name="attn",
    )(q, k, v, valid_row)


def gu_kernel(*refs):
    z_ref = refs[0]
    pieces = refs[1:-3]
    m_ref, w_s = refs[-2:]

    @pl.when(pl.program_id(1) == 0)
    def _():
        fill_rows(w_s, pieces[:len(pieces) // 2])
        fill_rows(w_s, pieces[len(pieces) // 2:], w_s.shape[1] // 2)

    t = m_ref.shape[1]
    sub = 256
    for r in range(0, z_ref.shape[0], sub):
        rows = pl.ds(r, sub)
        out = jnp.dot(z_ref[rows, :], w_s[...], preferred_element_type=F32).astype(BF16)
        a = out[:, :t].astype(F32)
        u = out[:, t:].astype(F32)
        m_ref[rows, :] = (a * jax.nn.sigmoid(a) * u).astype(BF16)


def gate_up(z, pieces, act, first_col, lo=0, hi=None):
    seq, dim = z.shape
    n_tiles = pieces[0].shape[1] // (2 * FF_TILE)
    hi = n_tiles if hi is None else hi
    cols = (hi - lo) * 2 * FF_TILE
    tm = 1024
    first = first_col // FF_TILE + lo
    ops = [z] + list(pieces) + list(pieces) + [act]
    return pl.pallas_call(
        gu_kernel,
        grid=(cols // (2 * FF_TILE), seq // tm),
        in_specs=[pl.BlockSpec((tm, dim), lambda n, m: (m, 0))]
        + [pl.BlockSpec((p.shape[0], FF_TILE), lambda n, m: (0, lo + n)) for p in pieces]
        + [pl.BlockSpec((p.shape[0], FF_TILE), lambda n, m: (0, n_tiles + lo + n)) for p in pieces]
        + [pl.BlockSpec(memory_space=pl.ANY)],
        out_specs=pl.BlockSpec((tm, FF_TILE), lambda n, m: (m, first + n)),
        out_shape=jax.ShapeDtypeStruct(act.shape, BF16),
        scratch_shapes=[pltpu.VMEM((dim, 2 * FF_TILE), BF16)],
        input_output_aliases={len(ops) - 1: 0},
        compiler_params=params(("arbitrary", "arbitrary")),
        cost_estimate=cost(2 * seq * dim * cols, seq * dim * 4),
        name="gate_up",
    )(*ops)


def down_kernel(plan, act_ref, *refs):
    n_w = sum(len(p) for p in plan)
    w_refs = refs[:n_w]
    out_ref, w_s, sems = refs[-3:]
    j, m = pl.program_id(0), pl.program_id(1)

    def copies(t):
        at = sum(len(p) for p in plan[:t])
        slot = t % 2
        return [pltpu.make_async_copy(w_refs[at + i], w_s.at[slot, pl.ds(row, w_refs[at + i].shape[0]), pl.ds(col, w_refs[at + i].shape[1])],
                                      sems.at[slot, i]) for i, (row, col) in enumerate(plan[t])]

    for t in range(len(plan)):
        @pl.when(jnp.logical_and(j == t, m == 0))
        def _(t=t):
            if t == 0:
                for c in copies(0):
                    c.start()
            for c in copies(t):
                c.wait()
            if t + 1 < len(plan):
                for c in copies(t + 1):
                    c.start()

    slot = lax.rem(j, 2)
    sub = 256
    for r in range(0, out_ref.shape[0], sub):
        rows = pl.ds(r, sub)
        out_ref[rows, :] = jnp.dot(act_ref[rows, :], w_s[slot], preferred_element_type=F32).astype(BF16)


def down(act, pairs, n_cols=None, first=0, buf=None):
    seq, kdim = act.shape
    blk = pairs[0][0][0].shape[1]
    tm = 512
    plan, ws = [], []
    for pair in pairs:
        spots = []
        for side, group in enumerate(pair):
            row = 0
            for p in group:
                spots.append((row, side * blk))
                ws.append(p)
                row += p.shape[0]
        plan.append(spots)
    n_cols = n_cols or 2 * blk * len(pairs)
    aliased = 0 if buf is None else 1
    ops = [act] + ws + ([buf] if aliased else [])
    return pl.pallas_call(
        functools.partial(down_kernel, plan),
        grid=(len(pairs), seq // tm),
        in_specs=[pl.BlockSpec((tm, kdim), lambda j, m: (m, 0))] + [pl.BlockSpec(memory_space=pl.ANY)] * (len(ws) + aliased),
        out_specs=pl.BlockSpec((tm, 2 * blk), lambda j, m: (m, first + j)),
        out_shape=jax.ShapeDtypeStruct((seq, n_cols), BF16),
        scratch_shapes=[pltpu.VMEM((2, kdim, 2 * blk), BF16), pltpu.SemaphoreType.DMA((2, 4))],
        input_output_aliases={len(ops) - 1: 0} if aliased else {},
        compiler_params=params(("arbitrary", "arbitrary")),
        cost_estimate=cost(2 * seq * kdim * 2 * blk * len(pairs), seq * kdim * 2),
        name="down",
    )(*ops)


def add_kernel(n_tot, idx_ref, x_ref, *refs):
    tots, y_ref = refs[:n_tot], refs[-1]
    blk = x_ref.shape[1] // N_PIECES
    j = 0
    for t in tots:
        for c in range(0, t.shape[1], blk):
            spot = pl.ds(pl.multiple_of(idx_ref[j] * blk, blk), blk)
            y_ref[:, spot] = (x_ref[:, spot].astype(F32) + t[:, c:c + blk].astype(F32)).astype(BF16)
            j += 1


def residual(x, totals, idx, y, prompt, seq):
    rows, dim = x.shape
    tm = 512
    n_m = seq // tm
    aliased = 0 if y is None else 1
    spot = lambda m, p: (prompt * n_m + m, 0)
    return pl.pallas_call(
        functools.partial(add_kernel, len(totals)),
        grid_spec=pltpu.PrefetchScalarGridSpec(
            num_scalar_prefetch=1, grid=(n_m,),
            in_specs=[pl.BlockSpec((tm, dim), spot)]
            + [pl.BlockSpec((tm, t.shape[1]), lambda m, p: (m, 0)) for t in totals]
            + [pl.BlockSpec(memory_space=pl.ANY)] * aliased,
            out_specs=pl.BlockSpec((tm, dim), spot)),
        out_shape=jax.ShapeDtypeStruct((rows, dim), BF16),
        input_output_aliases={2 + len(totals): 0} if aliased else {},
        compiler_params=params(("arbitrary",)),
        cost_estimate=cost(5e9, seq * dim * 6),
        name="residual",
    )(idx, x, *totals, *([y] if aliased else []))


def rope_tables(seq_len, head_dim):
    half = head_dim // 2
    inv_freq = 10000.0 ** (-2.0 * jnp.arange(half, dtype=F32) / head_dim)
    angles = jnp.arange(seq_len, dtype=F32)[:, None] * inv_freq[None, :]
    return jnp.cos(angles), jnp.sin(angles)


def solution(mesh):
    n_wg = mesh.shape['wg']
    batch_spec = P(('dp', 'wg'), None, None)
    in_specs = (batch_spec, P(('dp', 'wg'), None), P(None), P('wg', 'tp'), P('wg', None),
                P('wg', 'tp'), P('wg', 'tp'), P('tp', 'wg'), P('tp', 'wg'))
    out_specs = (batch_spec, batch_spec, batch_spec)
    to_right = [(i, (i + 2) % n_wg) for i in range(n_wg)]
    to_left = [(i, (i - 2) % n_wg) for i in range(n_wg)]
    far_right = [(i, (i + 4) % n_wg) for i in range(n_wg)]
    far_left = [(i, (i - 4) % n_wg) for i in range(n_wg)]
    to_pair = [(i, i ^ 1) for i in range(n_wg)]

    def shift(val, pairs):
        return lax.ppermute(val, 'wg', pairs)

    def halves(v):
        return v[:v.shape[0] // 2], v[v.shape[0] // 2:]

    def spread(shard):
        top, bottom = halves(shard)
        out = []
        for v, pairs in ((shard, to_right), (shard, to_left), (top, far_right), (bottom, far_left)):
            out.append(shift(v, pairs))
        return tuple(out)

    def swaps(vals):
        out = []
        for v in vals:
            out.append(shift(v, to_pair))
        return tuple(out)


    def ring_one(top, bottom):
        out = []
        for v, pairs in ((top, to_right), (bottom, to_left), (bottom, to_right), (top, to_left)):
            out.append(shift(v, pairs))
        return tuple(out)

    def ring_two(got):
        top = shift(got[0], to_right)
        bottom = shift(got[1], to_left)
        return top, bottom


    def local_step(x_in, valid, ln_gain, w_q, w_kv, w_gate, w_up, w_o, w_down):
        n_prompts, seq, dim = x_in.shape
        hd = w_kv.shape[1] // 2
        ff = w_gate.shape[1]
        me = lax.axis_index('wg')
        chip, core = me // 2, me % 2
        n_chip = n_wg // 2
        order = []
        for step in (0, -1, 1, 2):
            c = (chip + step + n_chip) % n_chip
            order += [2 * c + core, 2 * c + 1 - core]
        idx = jnp.stack(order).astype(jnp.int32)
        block = jnp.arange(n_wg, dtype=jnp.int32)
        away = (block // 2 - chip + n_chip) % n_chip
        slot = jnp.where(away == 0, 0, jnp.where(away == n_chip - 1, 1, jnp.where(away == 1, 2, 3)))
        pos = 2 * slot + (block % 2 != core).astype(jnp.int32)

        x2 = x_in.reshape(n_prompts * seq, dim)
        oc = w_o.shape[0]
        cut_at = 5 * FF_TILE

        def chunk(gate, up, lo, hi):
            pair = [gate[:, lo:hi], up[:, lo:hi]]
            return tuple(jnp.concatenate([halves(v)[i] for v in pair], axis=1) for i in range(2))

        def tie(vals, *deps):
            return lax.optimization_barrier(tuple(vals) + deps)[:len(vals)]

        def k_pieces(own, got):
            sw = swaps((own,) + got)
            return [own, sw[0], got[0], sw[1], got[1], sw[2], got[2], got[3], sw[3], sw[4]]

        def ring_pieces(near, sw_near, far, sw_far):
            out = []
            for i, j in ((0, 1), (2, 4), (5, 3)):
                out += [near[i], near[j], sw_near[i], sw_near[j]]
            return out + list(far) + list(sw_far)

        s_q = jnp.concatenate([w_q, w_kv], axis=1)
        got_q = spread(s_q)
        cos_t, sin_t = rope_tables(seq, hd)
        valid_col = valid.reshape(-1, 1)
        valid_row = valid.reshape(n_prompts, 1, seq)

        z0 = layer_norm(after(x2, s_q), ln_gain, pos, 0, seq)
        s_a = chunk(*tie([w_gate, w_up], z0), 0, cut_at)
        one_a = ring_one(*s_a)
        got_q = tie(got_q, *s_a)
        p_q = k_pieces(s_q, got_q)
        z1 = layer_norm(after(x2, *got_q), ln_gain, pos, 1, seq)
        s_b = chunk(*tie([w_gate, w_up], z1), cut_at, ff)
        q0, k_cache, v_cache, v0 = qkv(after(z0, *s_b), p_q, cos_t, sin_t, valid_col, hd, 0, ())
        act0 = attention(q0, k_cache, v0, valid_row, 0, oc + ff)

        near_a = tie(s_a + one_a, act0)
        far_a = ring_two(near_a[2:])
        sw_near = swaps(near_a)
        q1, k_cache, v_cache, v1 = qkv(after(z1, *near_a), p_q, cos_t, sin_t, valid_col, hd, 1,
                                          (k_cache, v_cache))
        s_b = tie(s_b, q1)
        one_b = ring_one(*s_b)
        far_a = tie(far_a, *s_b)
        p_a = ring_pieces(near_a, sw_near, far_a, swaps(far_a))
        act0 = gate_up(z0, p_a, act0, oc, 0, 3)

        near_b = tie(s_b + one_b, act0)
        far_b = ring_two(near_b[2:])
        sw_near = swaps(near_b)
        act0 = gate_up(z0, p_a, after(act0, *near_b), oc, 3, None)
        top_d, bottom_d = tie(halves(jnp.concatenate(tie([w_o, w_down], q1), axis=0)), act0)
        one_d = ring_one(top_d, bottom_d)
        far_b = tie(far_b, act0)
        p_b = ring_pieces(near_b, sw_near, far_b, swaps(far_b))
        own_d = swaps((top_d, bottom_d))
        act0 = gate_up(z0, p_b, act0, oc + cut_at)

        pair_0 = ([top_d, bottom_d], list(own_d))
        part_a = down(act0, [pair_0])
        tot_a = lax.psum(part_a, 'tp')
        one_d = tie(one_d, part_a)
        far_d = ring_two(one_d)
        sw_near = swaps(one_d)
        near = [([one_d[0], one_d[2]], [sw_near[0], sw_near[2]]), ([one_d[3], one_d[1]], [sw_near[3], sw_near[1]])]
        part_b = down(after(act0, *one_d), near, dim - part_a.shape[1])
        far_d = tie(far_d, part_b)
        sw_far = swaps(far_d)
        pair_3 = (list(far_d), list(sw_far))
        part_b = down(act0, [pair_3], dim - part_a.shape[1], 2, part_b)
        tot_b = lax.psum(after(part_b, tot_a), 'tp')

        act1 = attention(after(q1, part_b), k_cache, v1, valid_row, 1, oc + ff)
        act1 = gate_up(z1, p_a, act1, oc)
        act1 = gate_up(z1, p_b, act1, oc + cut_at)
        part_c = down(act1, [pair_0] + near + [pair_3])
        tot_c = lax.psum(after(part_c, tot_b), 'tp')

        y = residual(x2, [tot_a, tot_b], idx, None, 0, seq)
        y = residual(x2, [tot_c], idx, y, 1, seq)
        out3 = lambda v: v.reshape(n_prompts, seq, v.shape[-1])
        return out3(y), out3(k_cache), out3(v_cache)

    return jax.shard_map(local_step, mesh=mesh, in_specs=in_specs, out_specs=out_specs, check_vma=False)
```

time: 763 us -> 694 us (0.910)
  Pallas kernels: 0 us -> 402 us
  matrix products: 367 us -> 0 us
  waiting for transfers between devices: 288 us -> 212 us
  other arithmetic: 56.6 us -> 9.23 us
  starting transfers between devices: 0.44 us -> 40 us
  local copies, waits for them, and re-layouts: 33.1 us -> 11.5 us
    pallas_call x0 -> x17, Pallas kernels: none -> 402 us  [the longest x5 178 us: gate_up(): pl.pallas_call(gu_kernel, grid=(cols // (2 * FF_TILE), seq // tm), in_spe...]
    dot_general x7 -> x0, matrix products: 337 us -> none  [the longest x1 86.9 us: local_step(): jnp.einsum('bsk,kd->bsd', mlp_out, wdown_full, preferred_element_type=jnp...]
    psum x1 -> x3, waiting for transfers between devices: 285 us -> 144 us  [the longest x1 144 us: local_step(): tot_c = lax.psum(after(part_c, tot_b), 'tp')]
    ppermute x0 -> x51, waiting for transfers between devices: none -> 67.5 us  [shift(): return lax.ppermute(val, 'wg', pairs)]
    ppermute x0 -> x51, starting transfers between devices: none -> 39.8 us  [shift(): return lax.ppermute(val, 'wg', pairs)]
    sub x1 -> x0, matrix products: 30.3 us -> none  [attend_and_mix(): probs = jax.nn.softmax(scores, axis=-1).astype(jnp.bfloat16)]
    unnamed x42 -> x49, local copies, waits for them, and re-layouts: 27.2 us -> 4.49 us
    convert_element_type x1 -> x0, other arithmetic: 19.9 us -> none  [local_step(): (x_in.astype(jnp.float32) + total.astype(jnp.float32)).astype(jnp.bfloat16)]
  transfers between devices with their start and end apart: 7 -> 54, of which waited for: 1 -> 16; matrix products, arithmetic and copies ran while one was open for 45% -> 2% of each run, Pallas kernels for 0% -> 57%
where the time goes in v1:
time: 694 us; the launch traced here: 689 us
  Pallas kernels  402 us (58%)
  waiting for transfers between devices  212 us (31%)
  starting transfers between devices  40 us (6%)
  between operations  14.7 us (2%)
  local copies, waits for them, and re-layouts  11.5 us (2%)
  other arithmetic  9.23 us (1%)
    pallas_call x5, Pallas kernels, gate_up(): pl.pallas_call(gu_kernel, grid=(cols // (2 * FF_TILE), seq // tm), in_spe...  178 us
    psum x1, waiting for transfers between devices, local_step(): tot_c = lax.psum(after(part_c, tot_b), 'tp')  144 us
    pallas_call x4, Pallas kernels, down(): pl.pallas_call(functools.partial(down_kernel, plan), grid=(len(pairs), se...  110 us
    ppermute x51, waiting for transfers between devices, shift(): return lax.ppermute(val, 'wg', pairs)  67.5 us
    ppermute x51, starting transfers between devices, shift(): return lax.ppermute(val, 'wg', pairs)  39.8 us
    pallas_call x2, Pallas kernels, attention(): pl.pallas_call(functools.partial(attn_kernel, n_blk, hd ** (-0.5)), grid=...  37.3 us
    pallas_call x2, Pallas kernels, qkv(): pl.pallas_call(functools.partial(qkv_kernel, n_heads, hd, len(caches)), g...  29.9 us
    pallas_call x2, Pallas kernels, layer_norm(): pl.pallas_call(ln_kernel, grid_spec=pltpu.PrefetchScalarGridSpec(num_scal...  25.5 us
  transfers between devices with their start and end apart: 54, of which 16 were waited for; matrix products, arithmetic and copies ran while one was open for 2% of the time, Pallas kernels for 57%

profile of v1, /device:TPU:97, one launch (start us, length us, event | category | flops | bytes accessed | tf_op | source)
XLA Modules:
  0.0 688.8 jit_solution(8198911070063245324)
XLA Ops:
  18.8 12.9 %ln.2.refs_0_ = bf16[2048,2048]{1,0:T(8,128)(2,1)} custom-call(s32[8]{0:T(128)} %fusion.2.pos_ref, bf16[4096,2048]{1,0:T(8,128)(2,1)} %bitcast.17, f32[1,2048]{1,0:T(1,128)} %bitcast.26), custom_call_target="tpu_custom_call" | custom-call | flops 5000000000 | bytes 16777216 | tf_op jit(solution)/shard_map/ln/pallas_call | solution.py:52
  36.8 4.8 fusion
  42.9 12.7 %ln.3.refs_0_ = bf16[2048,2048]{1,0:T(8,128)(2,1)} custom-call(s32[8]{0:T(128)} %fusion.2.pos_ref, bf16[4096,2048]{1,0:T(8,128)(2,1)} %bitcast.18, f32[1,2048]{1,0:T(1,128)} %bitcast.27), custom_call_target="tpu_custom_call" | custom-call | flops 5000000000 | bytes 16777216 | tf_op jit(solution)/shard_map/ln/pallas_call | solution.py:52
  62.6 2.9 collective-permute-start.7
  65.5 14.9 %qkv.2 = (bf16[2048,512]{1,0:T(8,128)(2,1)}, bf16[4096,256]{1,0:T(8,128)(2,1)}, bf16[4096,256]{1,0:T(8,128)(2,1)}, bf16[2048,256]{1,0:T(8,128)(2,1)}) custom-call(bf16[2048,2048]{1,0:T(8,128)(2,1)} %ln.2.refs_0_, f32[2048,128]{1,0:T(8,128)} %get-tuple-element.122.refs_1_, f32[2048,128]{1,0:T(8,128)} %get-tuple-element.121.refs_2_, s32[4096,1]{1,0:T(8,128)} %bitcast.22, ...), custom_call_target="tpu_custom_call" | custom-call | flops 8589934592 | bytes 16777216 | tf_op jit(solution)/shard_map/qkv/pallas_call | solution.py:119
  80.4 18.7 %attn.2.refs_33_ = bf16[2048,4608]{1,0:T(8,128)(2,1)} custom-call(bf16[2048,512]{1,0:T(8,128)(2,1)} %get-tuple-element.67.q_ref, bf16[4096,256]{1,0:T(8,128)(2,1)} %get-tuple-element.68.k_ref.refs_14_, bf16[2048,256]{1,0:T(8,128)(2,1)} %get-tuple-element.69.v_ref, s32[2,1,2048]{2,1,0:T(1,128)} %reshape.36.valid_ref), custom_call_target="tpu_custom_call" | custom-call | flops 16000000000 | bytes 6291456 | tf_op jit(solution)/shard_map/attn/pallas_call | solution.py:177
  99.1 20.2 %collective-permute-done.6.refs_6_.refs_22_ = bf16[128,5120]{1,0:T(8,128)(2,1)} collective-permute-done((bf16[128,5120]{1,0:T(8,128)(2,1)S(1)}, bf16[128,5120]{1,0:T(8,128)(2,1)}, u32[]{:S(2)}, u32[]{:S(2)}) %collective-permute-start.6) | collective-permute-done | bytes 1310752 | tf_op jit(solution)/shard_map/ppermute | solution.py:352
  119.2 3.1 collective-permute-start.24
  124.6 15.0 %qkv.3 = (bf16[2048,512]{1,0:T(8,128)(2,1)}, bf16[4096,256]{1,0:T(8,128)(2,1)}, bf16[4096,256]{1,0:T(8,128)(2,1)}, bf16[2048,256]{1,0:T(8,128)(2,1)}) custom-call(bf16[2048,2048]{1,0:T(8,128)(2,1)} %ln.3.refs_0_, f32[2048,128]{1,0:T(8,128)} %get-tuple-element.122.refs_1_, ...), custom_call_target="tpu_custom_call", output_to_operand_aliasing={{1}: (14, {}), {2}: (15, {})} | custom-call | flops 8589934592 | bytes 16777216 | tf_op jit(solution)/shard_map/qkv/pallas_call | solution.py:119
  139.7 10.2 %collective-permute-done.23.refs_13_.refs_29_ = bf16[128,5120]{1,0:T(8,128)(2,1)} collective-permute-done((bf16[128,5120]{1,0:T(8,128)(2,1)}, bf16[128,5120]{1,0:T(8,128)(2,1)}, u32[]{:S(2)}, u32[]{:S(2)}) %collective-permute-start.23) | collective-permute-done | bytes 1310752 | tf_op jit(solution)/shard_map/ppermute | solution.py:352
  162.5 33.6 %gate_up.5.refs_33_ = bf16[2048,4608]{1,0:T(8,128)(2,1)} custom-call(bf16[2048,2048]{1,0:T(8,128)(2,1)} %ln.2.refs_0_, bf16[128,5120]{1,0:T(8,128)(2,1)} %copy-done, bf16[128,5120]{1,0:T(8,128)(2,1)} %copy-done.1, bf16[128,5120]{1,0:T(8,128)(2,1)} %collective-permute-done.17.refs_3_.refs_19_, ...), custom_call_target="tpu_custom_call", output_to_operand_aliasing={{}: (33, {})} | custom-call | flops 25769803776 | bytes 16777216 | tf_op jit(solution)/shard_map/gate_up/pallas_call | solution.py:220
  199.1 17.3 %collective-permute-done.33.refs_13_.refs_29_ = bf16[128,3072]{1,0:T(8,128)(2,1)} collective-permute-done((bf16[128,3072]{1,0:T(8,128)(2,1)}, bf16[128,3072]{1,0:T(8,128)(2,1)}, u32[]{:S(2)}, u32[]{:S(2)}) %collective-permute-start.33) | collective-permute-done | bytes 786464 | tf_op jit(solution)/shard_map/ppermute | solution.py:352
  216.6 23.9 %gate_up.6.refs_33_ = bf16[2048,4608]{1,0:T(8,128)(2,1)} custom-call(bf16[2048,2048]{1,0:T(8,128)(2,1)} %ln.2.refs_0_, bf16[128,5120]{1,0:T(8,128)(2,1)} %copy-done, bf16[128,5120]{1,0:T(8,128)(2,1)} %copy-done.1, bf16[128,5120]{1,0:T(8,128)(2,1)} %collective-permute-done.17.refs_3_.refs_19_, ...), custom_call_target="tpu_custom_call", output_to_operand_aliasing={{}: (33, {})} | custom-call | flops 17179869184 | bytes 16777216 | tf_op jit(solution)/shard_map/gate_up/pallas_call | solution.py:220
  253.5 33.5 %gate_up.7.act_ref = bf16[2048,4608]{1,0:T(8,128)(2,1)} custom-call(bf16[2048,2048]{1,0:T(8,128)(2,1)} %ln.2.refs_0_, bf16[128,3072]{1,0:T(8,128)(2,1)} %pad_maximum_fusion.3.refs_1_.refs_17_, bf16[128,3072]{1,0:T(8,128)(2,1)} %pad_maximum_fusion.4.refs_2_.refs_18_, ...), custom_call_target="tpu_custom_call", output_to_operand_aliasing={{}: (33, {})} | custom-call | flops 25769803776 | bytes 16777216 | tf_op jit(solution)/shard_map/gate_up/pallas_call | solution.py:220
  287.1 16.6 %down.4 = bf16[2048,512]{1,0:T(8,128)(2,1)} custom-call(bf16[2048,4608]{1,0:T(8,128)(2,1)} %gate_up.7.act_ref, bf16[2304,256]{1,0:T(8,128)(2,1)} %copy-done.10, bf16[2304,256]{1,0:T(8,128)(2,1)} %copy-done.9, bf16[2304,256]{1,0:T(8,128)(2,1)} %copy-done.14, bf16[2304,256]{1,0:T(8,128)(2,1)} %collective-permute-done.42.refs_3_), custom_call_target="tpu_custom_call" | custom-call | flops 9663676416 | bytes 18874368 | tf_op jit(solution)/shard_map/down/pallas_call | solution.py:285
  312.0 27.6 %down.5.refs_4_ = bf16[2048,1536]{1,0:T(8,128)(2,1)} custom-call(bf16[2048,4608]{1,0:T(8,128)(2,1)} %gate_up.7.act_ref, bf16[2304,256]{1,0:T(8,128)(2,1)} %collective-permute-done.37.refs_0_.refs_4_, bf16[2304,256]{1,0:T(8,128)(2,1)} %collective-permute-done.39.refs_1_.refs_5_, bf16[2304,256]{1,0:T(8,128)(2,1)} %copy-done.15, ...), custom_call_target="tpu_custom_call" | custom-call | flops 19327352832 | bytes 18874368 | tf_op jit(solution)/shard_map/down/pallas_call | solution.py:285
  344.5 16.7 %down.6 = bf16[2048,1536]{1,0:T(8,128)(2,1)} custom-call(bf16[2048,4608]{1,0:T(8,128)(2,1)} %gate_up.7.act_ref, bf16[2304,256]{1,0:T(8,128)(2,1)} %copy-done.5, bf16[2304,256]{1,0:T(8,128)(2,1)} %copy-done.6, bf16[2304,256]{1,0:T(8,128)(2,1)} %copy-done.7, ...), custom_call_target="tpu_custom_call", output_to_operand_aliasing={{}: (5, {})} | custom-call | flops 9663676416 | bytes 18874368 | tf_op jit(solution)/shard_map/down/pallas_call | solution.py:285
  361.4 18.7 %attn.3.refs_33_ = bf16[2048,4608]{1,0:T(8,128)(2,1)} custom-call(bf16[2048,512]{1,0:T(8,128)(2,1)} %get-tuple-element.103.q_ref, bf16[4096,256]{1,0:T(8,128)(2,1)} %get-tuple-element.104.k_ref, bf16[2048,256]{1,0:T(8,128)(2,1)} %get-tuple-element.105.v_ref, s32[2,1,2048]{2,1,0:T(1,128)} %reshape.36.valid_ref), custom_call_target="tpu_custom_call" | custom-call | flops 16000000000 | bytes 6291456 | tf_op jit(solution)/shard_map/attn/pallas_call | solution.py:177
  380.0 53.1 %gate_up.8.refs_33_ = bf16[2048,4608]{1,0:T(8,128)(2,1)} custom-call(bf16[2048,2048]{1,0:T(8,128)(2,1)} %ln.3.refs_0_, bf16[128,5120]{1,0:T(8,128)(2,1)} %copy-done, bf16[128,5120]{1,0:T(8,128)(2,1)} %copy-done.1, bf16[128,5120]{1,0:T(8,128)(2,1)} %collective-permute-done.17.refs_3_.refs_19_, ...), custom_call_target="tpu_custom_call", output_to_operand_aliasing={{}: (33, {})} | custom-call | flops 42949672960 | bytes 16777216 | tf_op jit(solution)/shard_map/gate_up/pallas_call | solution.py:220
  433.1 34.0 %gate_up.9.act_ref = bf16[2048,4608]{1,0:T(8,128)(2,1)} custom-call(bf16[2048,2048]{1,0:T(8,128)(2,1)} %ln.3.refs_0_, bf16[128,3072]{1,0:T(8,128)(2,1)} %pad_maximum_fusion.3.refs_1_.refs_17_, bf16[128,3072]{1,0:T(8,128)(2,1)} %pad_maximum_fusion.4.refs_2_.refs_18_, ...), custom_call_target="tpu_custom_call", output_to_operand_aliasing={{}: (33, {})} | custom-call | flops 25769803776 | bytes 16777216 | tf_op jit(solution)/shard_map/gate_up/pallas_call | solution.py:220
  467.1 49.6 %down.7 = bf16[2048,2048]{1,0:T(8,128)(2,1)} custom-call(bf16[2048,4608]{1,0:T(8,128)(2,1)} %gate_up.9.act_ref, bf16[2304,256]{1,0:T(8,128)(2,1)} %copy-done.10, bf16[2304,256]{1,0:T(8,128)(2,1)} %copy-done.9, bf16[2304,256]{1,0:T(8,128)(2,1)} %copy-done.14, bf16[2304,256]{1,0:T(8,128)(2,1)} %collective-permute-done.42.refs_3_, ...), custom_call_target="tpu_custom_call" | custom-call | flops 38654705664 | bytes 18874368 | tf_op jit(solution)/shard_map/down/pallas_call | solution.py:285
  517.5 10.3 %residual.2.refs_1_ = bf16[4096,2048]{1,0:T(8,128)(2,1)} custom-call(s32[8]{0:T(128)} %stack.35.idx_ref, bf16[4096,2048]{1,0:T(8,128)(2,1)} %bitcast.19, bf16[2048,512]{1,0:T(8,128)(2,1)} %all-reduce.4.cloned.1.call-done.refs_0_, bf16[2048,1536]{1,0:T(8,128)(2,1)} %all-reduce.6.cloned.1.call-done.refs_1_), custom_call_target="tpu_custom_call" | custom-call | flops 5000000000 | bytes 25165824 | tf_op jit(solution)/shard_map/residual/pallas_call | solution.py:316
  527.9 143.8 %all-reduce.8.cloned.1.call-done.refs_0_ = bf16[2048,2048]{1,0:T(8,128)(2,1)} async-done(((bf16[2048,2048]{1,0:T(8,128)(2,1)}), bf16[2048,2048]{1,0:T(8,128)(2,1)}) %all-reduce.8.cloned.1.call-update) | async-done | bytes 8388624 | tf_op jit(solution)/shard_map/psum | solution.py:477
  671.7 10.2 %residual.3 = bf16[4096,2048]{1,0:T(8,128)(2,1)} custom-call(s32[8]{0:T(128)} %stack.35.idx_ref, bf16[4096,2048]{1,0:T(8,128)(2,1)} %bitcast.20, bf16[2048,2048]{1,0:T(8,128)(2,1)} %all-reduce.8.cloned.1.call-done.refs_0_, bf16[4096,2048]{1,0:T(8,128)(2,1)} %residual.2.refs_1_), custom_call_target="tpu_custom_call", output_to_operand_aliasing={{}: (3, {})} | custom-call | flops 5000000000 | bytes 25165824 | tf_op jit(solution)/shard_map/residual/pallas_call | solution.py:316
  (168 shorter events, 70.1 us)
Async XLA Ops:
  7.2 354.1 %all-reduce.4.cloned.1.call-start = ((), (), s32[]{:S(2)}) async-start(), calls=%async_computation | async-start | bytes 4194304 | tf_op jit(solution)/shard_map/psum | solution.py:461
  13.1 46.8 %collective-permute-start.8 = (bf16[256,1024]{1,0:T(8,128)(2,1)S(1)}, bf16[256,1024]{1,0:T(8,128)(2,1)}, u32[]{:S(2)}, u32[]{:S(2)}) collective-permute-start(bf16[256,1024]{1,0:T(8,128)(2,1)S(1)} %constant_dynamic-update-slice_fusion.refs_4_), channel_id=1, source_target_pairs={{0,1},{1,0},{2,3},{3,2},{4,5},{5,4},{6,7},{7,6},{8,9},{9,8},{10,11... | collective-permute-start | bytes 1572872 | tf_op jit(solution)/shard_map/ppermute | solution.py:352
  59.9 39.2 %collective-permute-start.4 = (bf16[128,5120]{1,0:T(8,128)(2,1)S(1)}, bf16[128,5120]{1,0:T(8,128)(2,1)}, u32[]{:S(2)}, u32[]{:S(2)}) collective-permute-start(bf16[128,5120]{1,0:T(8,128)(2,1)S(1)} %pad_maximum_fusion.refs_1_.refs_17_), channel_id=1, source_target_pairs={{0,2},{1,3},{2,4},{3,5},{4,6},{5,7},{6,0},{7,1},{8,10},{9,11},{10,... | collective-permute-start | bytes 3932168 | tf_op jit(solution)/shard_map/ppermute | solution.py:352
  59.9 39.2 %collective-permute-start.5 = (bf16[128,5120]{1,0:T(8,128)(2,1)S(1)}, bf16[128,5120]{1,0:T(8,128)(2,1)}, u32[]{:S(2)}, u32[]{:S(2)}) collective-permute-start(bf16[128,5120]{1,0:T(8,128)(2,1)S(1)} %pad_maximum_fusion.1.refs_2_.refs_18_), channel_id=1, source_target_pairs={{0,6},{1,7},{2,0},{3,1},{4,2},{5,3},{6,4},{7,5},{8,14},{9,15},{10,... | collective-permute-start | bytes 3932168 | tf_op jit(solution)/shard_map/ppermute | solution.py:352
  62.6 56.7 %collective-permute-start.6 = (bf16[128,5120]{1,0:T(8,128)(2,1)S(1)}, bf16[128,5120]{1,0:T(8,128)(2,1)}, u32[]{:S(2)}, u32[]{:S(2)}) collective-permute-start(bf16[128,5120]{1,0:T(8,128)(2,1)S(1)} %pad_maximum_fusion.1.refs_2_.refs_18_), channel_id=1, source_target_pairs={{0,2},{1,3},{2,4},{3,5},{4,6},{5,7},{6,0},{7,1},{8,10},{9,11},{10,... | collective-permute-start | bytes 3932168 | tf_op jit(solution)/shard_map/ppermute | solution.py:352
  62.6 56.6 %collective-permute-start.7 = (bf16[128,5120]{1,0:T(8,128)(2,1)S(1)}, bf16[128,5120]{1,0:T(8,128)(2,1)}, u32[]{:S(2)}, u32[]{:S(2)}) collective-permute-start(bf16[128,5120]{1,0:T(8,128)(2,1)S(1)} %pad_maximum_fusion.refs_1_.refs_17_), channel_id=1, source_target_pairs={{0,6},{1,7},{2,0},{3,1},{4,2},{5,3},{6,4},{7,5},{8,14},{9,15},{10,... | collective-permute-start | bytes 3932168 | tf_op jit(solution)/shard_map/ppermute | solution.py:352
  119.2 32.7 %collective-permute-start.24 = (bf16[128,5120]{1,0:T(8,128)(2,1)}, bf16[128,5120]{1,0:T(8,128)(2,1)}, u32[]{:S(2)}, u32[]{:S(2)}) collective-permute-start(bf16[128,5120]{1,0:T(8,128)(2,1)} %collective-permute-done.5.refs_10_.refs_26_), channel_id=1, source_target_pairs={{0,6},{1,7},{2,0},{3,1},{4,2},{5,3},{6,4},{7,5},{8,14},{9,15},{10,... | collective-permute-start | bytes 3932168 | tf_op jit(solution)/shard_map/ppermute | solution.py:352
  155.0 41.1 %collective-permute-start.13 = (bf16[128,3072]{1,0:T(8,128)(2,1)S(1)}, bf16[128,3072]{1,0:T(8,128)(2,1)}, u32[]{:S(2)}, u32[]{:S(2)}) collective-permute-start(bf16[128,3072]{1,0:T(8,128)(2,1)S(1)} %copy-done.11), channel_id=1, source_target_pairs={{0,2},{1,3},{2,4},{3,5},{4,6},{5,7},{6,0},{7,1},{8,10},{9,11},{10,... | collective-permute-start | bytes 2359304 | tf_op jit(solution)/shard_map/ppermute | solution.py:352
  156.8 39.2 %collective-permute-start.14 = (bf16[128,3072]{1,0:T(8,128)(2,1)}, bf16[128,3072]{1,0:T(8,128)(2,1)}, u32[]{:S(2)}, u32[]{:S(2)}) collective-permute-start(bf16[128,3072]{1,0:T(8,128)(2,1)} %pad_maximum_fusion.4.refs_2_.refs_18_), channel_id=1, source_target_pairs={{0,6},{1,7},{2,0},{3,1},{4,2},{5,3},{6,4},{7,5},{8,14},{9,15},{10,... | collective-permute-start | bytes 2359304 | tf_op jit(solution)/shard_map/ppermute | solution.py:352
  158.6 37.5 %collective-permute-start.15 = (bf16[128,3072]{1,0:T(8,128)(2,1)}, bf16[128,3072]{1,0:T(8,128)(2,1)}, u32[]{:S(2)}, u32[]{:S(2)}) collective-permute-start(bf16[128,3072]{1,0:T(8,128)(2,1)} %pad_maximum_fusion.4.refs_2_.refs_18_), channel_id=1, source_target_pairs={{0,2},{1,3},{2,4},{3,5},{4,6},{5,7},{6,0},{7,1},{8,10},{9,11},{10,... | collective-permute-start | bytes 2359304 | tf_op jit(solution)/shard_map/ppermute | solution.py:352
  160.5 35.6 %collective-permute-start.16 = (bf16[128,3072]{1,0:T(8,128)(2,1)S(1)}, bf16[128,3072]{1,0:T(8,128)(2,1)}, u32[]{:S(2)}, u32[]{:S(2)}) collective-permute-start(bf16[128,3072]{1,0:T(8,128)(2,1)S(1)} %copy-done.11), channel_id=1, source_target_pairs={{0,6},{1,7},{2,0},{3,1},{4,2},{5,3},{6,4},{7,5},{8,14},{9,15},{10,... | collective-permute-start | bytes 2359304 | tf_op jit(solution)/shard_map/ppermute | solution.py:352
  197.9 44.6 %collective-permute-start.29 = (bf16[128,3072]{1,0:T(8,128)(2,1)}, bf16[128,3072]{1,0:T(8,128)(2,1)S(1)}, u32[]{:S(2)}, u32[]{:S(2)}) collective-permute-start(bf16[128,3072]{1,0:T(8,128)(2,1)} %collective-permute-done.13.refs_5_.refs_21_), channel_id=1, source_target_pairs={{0,1},{1,0},{2,3},{3,2},{4,5},{5,4},{6,7},{7,6},{8,9},{9,8},{10,11... | collective-permute-start | bytes 2359304 | tf_op jit(solution)/shard_map/ppermute | solution.py:352
  198.5 43.6 %collective-permute-start.27 = (bf16[128,3072]{1,0:T(8,128)(2,1)S(1)}, bf16[128,3072]{1,0:T(8,128)(2,1)}, u32[]{:S(2)}, u32[]{:S(2)}) collective-permute-start(bf16[128,3072]{1,0:T(8,128)(2,1)S(1)} %copy-done.11), channel_id=1, source_target_pairs={{0,1},{1,0},{2,3},{3,2},{4,5},{5,4},{6,7},{7,6},{8,9},{9,8},{10,11... | collective-permute-start | bytes 2359304 | tf_op jit(solution)/shard_map/ppermute | solution.py:352
  198.6 43.6 %collective-permute-start.28 = (bf16[128,3072]{1,0:T(8,128)(2,1)}, bf16[128,3072]{1,0:T(8,128)(2,1)}, u32[]{:S(2)}, u32[]{:S(2)}) collective-permute-start(bf16[128,3072]{1,0:T(8,128)(2,1)} %pad_maximum_fusion.4.refs_2_.refs_18_), channel_id=1, source_target_pairs={{0,1},{1,0},{2,3},{3,2},{4,5},{5,4},{6,7},{7,6},{8,9},{9,8},{10,11... | collective-permute-start | bytes 2359304 | tf_op jit(solution)/shard_map/ppermute | solution.py:352
  199.0 43.7 %collective-permute-start.30 = (bf16[128,3072]{1,0:T(8,128)(2,1)}, bf16[128,3072]{1,0:T(8,128)(2,1)}, u32[]{:S(2)}, u32[]{:S(2)}) collective-permute-start(bf16[128,3072]{1,0:T(8,128)(2,1)} %collective-permute-done.15.refs_6_.refs_22_), channel_id=1, source_target_pairs={{0,1},{1,0},{2,3},{3,2},{4,5},{5,4},{6,7},{7,6},{8,9},{9,8},{10,11... | collective-permute-start | bytes 2359304 | tf_op jit(solution)/shard_map/ppermute | solution.py:352
  245.7 58.0 %collective-permute-start.37 = (bf16[2304,256]{1,0:T(8,128)(2,1)S(1)}, bf16[2304,256]{1,0:T(8,128)(2,1)}, u32[]{:S(2)}, u32[]{:S(2)}) collective-permute-start(bf16[2304,256]{1,0:T(8,128)(2,1)S(1)} %get-tuple-element.94.refs_0_), channel_id=1, source_target_pairs={{0,2},{1,3},{2,4},{3,5},{4,6},{5,7},{6,0},{7,1},{8,10},{9,11},{10,... | collective-permute-start | bytes 3538952 | tf_op jit(solution)/shard_map/ppermute | solution.py:352
  247.1 56.5 %collective-permute-start.38 = (bf16[2304,256]{1,0:T(8,128)(2,1)S(1)}, bf16[2304,256]{1,0:T(8,128)(2,1)}, u32[]{:S(2)}, u32[]{:S(2)}) collective-permute-start(bf16[2304,256]{1,0:T(8,128)(2,1)S(1)} %get-tuple-element.95.refs_1_), channel_id=1, source_target_pairs={{0,6},{1,7},{2,0},{3,1},{4,2},{5,3},{6,4},{7,5},{8,14},{9,15},{10,... | collective-permute-start | bytes 3538952 | tf_op jit(solution)/shard_map/ppermute | solution.py:352
  248.3 55.3 %collective-permute-start.39 = (bf16[2304,256]{1,0:T(8,128)(2,1)S(1)}, bf16[2304,256]{1,0:T(8,128)(2,1)}, u32[]{:S(2)}, u32[]{:S(2)}) collective-permute-start(bf16[2304,256]{1,0:T(8,128)(2,1)S(1)} %get-tuple-element.95.refs_1_), channel_id=1, source_target_pairs={{0,2},{1,3},{2,4},{3,5},{4,6},{5,7},{6,0},{7,1},{8,10},{9,11},{10,... | collective-permute-start | bytes 3538952 | tf_op jit(solution)/shard_map/ppermute | solution.py:352
  248.6 55.1 %collective-permute-start.40 = (bf16[2304,256]{1,0:T(8,128)(2,1)S(1)}, bf16[2304,256]{1,0:T(8,128)(2,1)}, u32[]{:S(2)}, u32[]{:S(2)}) collective-permute-start(bf16[2304,256]{1,0:T(8,128)(2,1)S(1)} %get-tuple-element.94.refs_0_), channel_id=1, source_target_pairs={{0,6},{1,7},{2,0},{3,1},{4,2},{5,3},{6,4},{7,5},{8,14},{9,15},{10,... | collective-permute-start | bytes 3538952 | tf_op jit(solution)/shard_map/ppermute | solution.py:352
  252.0 35.0 %collective-permute-start.42 = (bf16[2304,256]{1,0:T(8,128)(2,1)S(1)}, bf16[2304,256]{1,0:T(8,128)(2,1)}, u32[]{:S(2)}, u32[]{:S(2)}) collective-permute-start(bf16[2304,256]{1,0:T(8,128)(2,1)S(1)} %get-tuple-element.95.refs_1_), channel_id=1, source_target_pairs={{0,1},{1,0},{2,3},{3,2},{4,5},{5,4},{6,7},{7,6},{8,9},{9,8},{10,11... | collective-permute-start | bytes 3538952 | tf_op jit(solution)/shard_map/ppermute | solution.py:352
  304.8 34.8 %collective-permute-start.43 = (bf16[2304,256]{1,0:T(8,128)(2,1)}, bf16[2304,256]{1,0:T(8,128)(2,1)S(1)}, u32[]{:S(2)}, u32[]{:S(2)}) collective-permute-start(bf16[2304,256]{1,0:T(8,128)(2,1)} %collective-permute-done.37.refs_0_.refs_4_), channel_id=1, source_target_pairs={{0,2},{1,3},{2,4},{3,5},{4,6},{5,7},{6,0},{7,1},{8,10},{9,11},{10,... | collective-permute-start | bytes 3538952 | tf_op jit(solution)/shard_map/ppermute | solution.py:352
  304.9 211.8 %all-reduce.6.cloned.1.call-start = ((), (), s32[]{:S(2)}) async-start(), calls=%async_computation.1 | async-start | bytes 12582912 | tf_op jit(solution)/shard_map/psum | solution.py:471
  306.9 32.8 %collective-permute-start.44 = (bf16[2304,256]{1,0:T(8,128)(2,1)}, bf16[2304,256]{1,0:T(8,128)(2,1)S(1)}, u32[]{:S(2)}, u32[]{:S(2)}) collective-permute-start(bf16[2304,256]{1,0:T(8,128)(2,1)} %collective-permute-done.38.refs_5_.refs_9_), channel_id=1, source_target_pairs={{0,6},{1,7},{2,0},{3,1},{4,2},{5,3},{6,4},{7,5},{8,14},{9,15},{10,... | collective-permute-start | bytes 3538952 | tf_op jit(solution)/shard_map/ppermute | solution.py:352
  361.3 310.4 %all-reduce.8.cloned.1.call-start = ((), (), s32[]{:S(2)}) async-start(), calls=%async_computation.2 | async-start | bytes 16777216 | tf_op jit(solution)/shard_map/psum | solution.py:477
  (53 other events, 917.6 us)
Sparse Core Ops, SparseCore 0:
  305.0 55.4 all-reduce.3
  362.9 121.5 all-reduce.5
  516.9 154.7 all-reduce.7

commit v2 on v1

--- a/solution.py
+++ b/solution.py
@@ -12,6 +12,7 @@
 BF16 = jnp.bfloat16
 N_PIECES = 8
 FF_TILE = 512
+CHIP_STEPS = (0, -1, 1, 2)
 VMEM_LIMIT = 60 * 1024 * 1024
 
 
@@ -136,34 +137,35 @@
     )(*ops)
 
 
-def attn_kernel(n_blk, scale, q_ref, k_ref, v_ref, valid_ref, o_ref):
-    i = pl.program_id(1)
+def attn_kernel(n_blk, scale, hd, q_ref, k_ref, v_ref, valid_ref, o_ref):
+    i = pl.program_id(0)
     blk = q_ref.shape[0]
     dn = (((1,), (1,)), ((), ()))
 
     def block(b):
         past = b * blk
-        q = q_ref[...]
-        s1 = lax.dot_general(q, k_ref[past:past + blk, :], dn, preferred_element_type=F32) * scale
         rows = lax.broadcasted_iota(jnp.int32, (blk, blk), 0)
         cols = lax.broadcasted_iota(jnp.int32, (blk, blk), 1)
         ok1 = jnp.logical_and(cols <= rows, valid_ref[:, past:past + blk] > 0)
-        s1 = jnp.where(ok1, s1, -1e30)
-        top = jnp.max(s1, axis=-1, keepdims=True)
-        if b:
-            s0 = lax.dot_general(q, k_ref[:past, :], dn, preferred_element_type=F32) * scale
-            s0 = jnp.where(valid_ref[:, :past] > 0, s0, -1e30)
-            top = jnp.maximum(top, jnp.max(s0, axis=-1, keepdims=True))
-            e0 = jnp.exp(s0 - top)
-        e1 = jnp.exp(s1 - top)
-        tot = jnp.sum(e1, axis=-1, keepdims=True)
-        if b:
-            tot = tot + jnp.sum(e0, axis=-1, keepdims=True)
-        inv = 1.0 / tot
-        out = jnp.dot((e1 * inv).astype(BF16), v_ref[past:past + blk, :], preferred_element_type=F32)
-        if b:
-            out = out + jnp.dot((e0 * inv).astype(BF16), v_ref[:past, :], preferred_element_type=F32)
-        o_ref[...] = out.astype(BF16)
+        for h in range(q_ref.shape[1] // hd):
+            q = q_ref[:, h * hd:(h + 1) * hd]
+            s1 = lax.dot_general(q, k_ref[past:past + blk, :], dn, preferred_element_type=F32) * scale
+            s1 = jnp.where(ok1, s1, -1e30)
+            top = jnp.max(s1, axis=-1, keepdims=True)
+            if b:
+                s0 = lax.dot_general(q, k_ref[:past, :], dn, preferred_element_type=F32) * scale
+                s0 = jnp.where(valid_ref[:, :past] > 0, s0, -1e30)
+                top = jnp.maximum(top, jnp.max(s0, axis=-1, keepdims=True))
+                e0 = jnp.exp(s0 - top)
+            e1 = jnp.exp(s1 - top)
+            tot = jnp.sum(e1, axis=-1, keepdims=True)
+            if b:
+                tot = tot + jnp.sum(e0, axis=-1, keepdims=True)
+            inv = 1.0 / tot
+            out = jnp.dot((e1 * inv).astype(BF16), v_ref[past:past + blk, :], preferred_element_type=F32)
+            if b:
+                out = out + jnp.dot((e0 * inv).astype(BF16), v_ref[:past, :], preferred_element_type=F32)
+            o_ref[:, h * hd:(h + 1) * hd] = out.astype(BF16)
 
     for b in range(n_blk):
         pl.when(i == b)(functools.partial(block, b))
@@ -171,19 +173,19 @@
 
 def attention(q, k, v, valid_row, prompt, act_cols):
     seq, hd = v.shape
-    n_heads = q.shape[1] // hd
+    q_cols = q.shape[1]
     blk = 512
     n_blk = seq // blk
     return pl.pallas_call(
-        functools.partial(attn_kernel, n_blk, hd ** -0.5),
-        grid=(n_heads, n_blk),
-        in_specs=[pl.BlockSpec((blk, hd), lambda h, i: (i, h)),
-                  pl.BlockSpec((seq, hd), lambda h, i: (prompt, 0)),
-                  pl.BlockSpec((seq, hd), lambda h, i: (0, 0)),
-                  pl.BlockSpec((None, 1, seq), lambda h, i: (prompt, 0, 0))],
-        out_specs=pl.BlockSpec((blk, hd), lambda h, i: (i, h)),
+        functools.partial(attn_kernel, n_blk, hd ** -0.5, hd),
+        grid=(n_blk,),
+        in_specs=[pl.BlockSpec((blk, q_cols), lambda i: (i, 0)),
+                  pl.BlockSpec((seq, hd), lambda i: (prompt, 0)),
+                  pl.BlockSpec((seq, hd), lambda i: (0, 0)),
+                  pl.BlockSpec((None, 1, seq), lambda i: (prompt, 0, 0))],
+        out_specs=pl.BlockSpec((blk, q_cols), lambda i: (i, 0)),
         out_shape=jax.ShapeDtypeStruct((seq, act_cols), BF16),
-        compiler_params=params(("arbitrary", "arbitrary")),
+        compiler_params=params(("arbitrary",)),
         cost_estimate=cost(16e9, seq * hd * 12),
         name="attn",
     )(q, k, v, valid_row)
@@ -296,14 +298,199 @@
     )(*ops)
 
 
+def ring_kernel(n_w, *refs):
+    act_ref, x_ref, w_refs, y_ref = refs[0], refs[1], refs[2:2 + n_w], refs[2 + n_w]
+    act_s, w_s, part, got, total, act_sem, w_sem, send_sem, recv_sem, out_sem = refs[3 + n_w:]
+    dim = x_ref.shape[1]
+    chip, core = lax.axis_index("wg") // 2, lax.axis_index("wg") % 2
+    n_chip = lax.axis_size("wg") // 2
+    n_pairs, _, seq, blk = part.shape
+    n_tp = lax.axis_size("tp")
+    d = lax.axis_index("tp")
+    quarter = seq // n_tp
+    n_steps = 2 * (n_tp - 1)
+    half_rows = act_s.shape[1]
+    per = n_w // n_pairs
+    k_half = w_refs[0].shape[0]
+
+    barrier = pltpu.get_barrier_semaphore()
+    for sg in (1, -1):
+        pl.semaphore_signal(barrier, inc=1, device_id={"tp": lax.rem(d + sg + n_tp, n_tp)},
+                            device_id_type=pl.DeviceIdType.MESH)
+    pl.semaphore_wait(barrier, 2)
+
+    def act_copy(i):
+        return pltpu.make_async_copy(act_ref.at[pl.ds(i * half_rows, half_rows), :], act_s.at[i], act_sem.at[i])
+
+    def w_copies(t):
+        out = []
+        for i in range(per):
+            side, row = i // 2, (i % 2) * k_half
+            dst = w_s.at[t % 2, pl.ds(row, k_half), pl.ds(side * blk, blk)]
+            out.append(pltpu.make_async_copy(w_refs[t * per + i], dst, w_sem.at[t % 2, i]))
+        return out
+
+    def rows_of(q):
+        return pl.ds(pl.multiple_of(lax.rem(q + 2 * n_tp, n_tp) * quarter, quarter), quarter)
+
+    def ring_copy(t, side, s):
+        sg = 1 - 2 * side
+        if s < n_tp - 1:
+            src, dst = part.at[t, side, rows_of(d - sg * s), :], got.at[t, side, s]
+        else:
+            rows = rows_of(d + sg * (n_tp - s))
+            src, dst = total.at[t, side, rows, :], total.at[t, side, rows, :]
+        return pltpu.make_async_remote_copy(
+            src_ref=src, dst_ref=dst, send_sem=send_sem.at[t, side, s], recv_sem=recv_sem.at[t, side, s],
+            device_id={"tp": lax.rem(d + sg + n_tp, n_tp)}, device_id_type=pl.DeviceIdType.MESH)
+
+    def x_copy(i, first):
+        return pltpu.make_async_copy(x_ref.at[pl.ds(first + i * half_rows, half_rows), :],
+                                     act_s.at[i, :, pl.ds(0, dim)], act_sem.at[i])
+
+    def place(t, side, k):
+        q = lax.rem(d + (1 - 2 * side) * (1 - k) + 2 * n_tp, n_tp)
+        here = lax.rem(chip + CHIP_STEPS[t] + n_chip, n_chip) * 2 + (core if side == 0 else 1 - core)
+        per_half = half_rows // quarter
+        return q, q // per_half, (q % per_half) * quarter, pl.multiple_of(here * blk, blk)
+
+    def out_copy(t, side, k):
+        q, h, row, col = place(t, side, k)
+        src = act_s.at[h, pl.ds(pl.multiple_of(row, quarter), quarter), pl.ds(col, blk)]
+        dst = y_ref.at[pl.ds(pl.multiple_of(y_ref.shape[0] - seq + q * quarter, quarter), quarter), pl.ds(col, blk)]
+        return pltpu.make_async_copy(src, dst, out_sem.at[t, side, k])
+
+    def finish(t, side, k):
+        q, h, row, col = place(t, side, k)
+
+        def add(i, carry):
+            at = i * 128
+            spot = (h, pl.ds(pl.multiple_of(row + at, 128), 128), pl.ds(col, blk))
+            tot = total[t, side, pl.ds(pl.multiple_of(q * quarter + at, 128), 128), :]
+            act_s[spot] = (act_s[spot].astype(F32) + tot.astype(F32)).astype(BF16)
+            return carry
+
+        lax.fori_loop(0, quarter // 128, add, 0)
+
+    def action(t, s):
+        for side in range(2):
+            sg = 1 - 2 * side
+            if s:
+                ring_copy(t, side, s - 1).wait_recv()
+            if 0 < s < n_tp:
+                q = lax.rem(d - sg * s + 2 * n_tp, n_tp) * quarter
+                into = part if s < n_tp - 1 else total
+
+                def add(i, carry, side=side, q=q, into=into):
+                    at = pl.multiple_of(i * 128, 128)
+                    rows = pl.ds(pl.multiple_of(q + at, 128), 128)
+                    into[t, side, rows, :] = (part[t, side, rows, :].astype(F32)
+                                              + got[t, side, s - 1, pl.ds(at, 128), :].astype(F32)).astype(BF16)
+                    return carry
+
+                lax.fori_loop(0, quarter // 128, add, 0)
+        for side in range(2):
+            if s < n_steps:
+                ring_copy(t, side, s).start()
+        if s >= n_tp - 1:
+            for side in range(2):
+                finish(t, side, s - (n_tp - 1))
+            for side in range(2):
+                out_copy(t, side, s - (n_tp - 1)).start()
+
+    for i in range(2):
+        act_copy(i).start()
+    for c in w_copies(0):
+        c.start()
+
+    def pair(t, carry):
+        for tt in range(n_pairs):
+            @pl.when(t == tt)
+            def _(tt=tt):
+                for c in w_copies(tt):
+                    c.wait()
+                if tt + 1 < n_pairs:
+                    for c in w_copies(tt + 1):
+                        c.start()
+        for i in range(2):
+            @pl.when(t == 0)
+            def _(i=i):
+                act_copy(i).wait()
+
+            def tile(r, c2, i=i):
+                at = pl.multiple_of(r * 256, 256)
+                out = jnp.dot(act_s[i, pl.ds(at, 256), :], w_s[lax.rem(t, 2)], preferred_element_type=F32).astype(BF16)
+                rows = pl.ds(pl.multiple_of(i * half_rows + at, 256), 256)
+                part[t, 0, rows, :] = out[:, :blk]
+                part[t, 1, rows, :] = out[:, blk:]
+                return c2
+
+            lax.fori_loop(0, half_rows // 256, tile, 0)
+
+            @pl.when(t > 0)
+            def _(i=i):
+                action(t - 1, 1 + i)
+        action(t, 0)
+        return carry
+
+    lax.fori_loop(0, n_pairs, pair, 0)
+    for i in range(2):
+        x_copy(i, y_ref.shape[0] - seq).start()
+    for i in range(2):
+        x_copy(i, y_ref.shape[0] - seq).wait()
+
+    state = [3] * (n_pairs - 1) + [1]
+    while min(state) <= n_steps:
+        for t in [n_pairs - 1] + list(range(n_pairs - 1)):
+            if state[t] <= n_steps and (t == n_pairs - 1 or state[t] <= state[-1] + 1):
+                action(t, state[t])
+                state[t] += 1
+
+    for t in range(n_pairs):
+        for side in range(2):
+            for s in range(n_steps):
+                ring_copy(t, side, s).wait_send()
+            for k in range(n_tp):
+                out_copy(t, side, k).wait()
+
+
+def down_ring(act, x, pairs):
+    seq, kdim = act.shape
+    ws = [p for pair in pairs for group in pair for p in group]
+    blk = ws[0].shape[1]
+    n_pairs = len(pairs)
+    n_tp = lax.axis_size("tp")
+    n_steps = 2 * (n_tp - 1)
+    shape = (n_pairs, 2, seq, blk)
+    return pl.pallas_call(
+        functools.partial(ring_kernel, len(ws)),
+        in_specs=[pl.BlockSpec(memory_space=pl.ANY)] * (2 + len(ws)),
+        out_specs=pl.BlockSpec(memory_space=pl.ANY),
+        out_shape=jax.ShapeDtypeStruct(x.shape, BF16),
+        scratch_shapes=[pltpu.VMEM((2, seq // 2, kdim), BF16), pltpu.VMEM((2, kdim, 2 * blk), BF16),
+                        pltpu.VMEM(shape, BF16), pltpu.VMEM((n_pairs, 2, n_tp - 1, seq // n_tp, blk), BF16),
+                        pltpu.VMEM(shape, BF16),
+                        pltpu.SemaphoreType.DMA((2,)), pltpu.SemaphoreType.DMA((2, len(ws) // n_pairs)),
+                        pltpu.SemaphoreType.DMA((n_pairs, 2, n_steps)), pltpu.SemaphoreType.DMA((n_pairs, 2, n_steps)),
+                        pltpu.SemaphoreType.DMA((n_pairs, 2, n_tp))],
+        compiler_params=pltpu.CompilerParams(collective_id=0, has_side_effects=True, vmem_limit_bytes=VMEM_LIMIT),
+        cost_estimate=cost(1.4e11, seq * kdim * 2),
+        name="down_ring",
+    )(act, x, *ws)
+
+
 def add_kernel(n_tot, idx_ref, x_ref, *refs):
     tots, y_ref = refs[:n_tot], refs[-1]
     blk = x_ref.shape[1] // N_PIECES
     j = 0
     for t in tots:
-        for c in range(0, t.shape[1], blk):
+        if len(t.shape) == 4:
+            parts = [t[i, side] for i in range(t.shape[0]) for side in range(2)]
+        else:
+            parts = [t[:, c:c + blk] for c in range(0, t.shape[1], blk)]
+        for v in parts:
             spot = pl.ds(pl.multiple_of(idx_ref[j] * blk, blk), blk)
-            y_ref[:, spot] = (x_ref[:, spot].astype(F32) + t[:, c:c + blk].astype(F32)).astype(BF16)
+            y_ref[:, spot] = (x_ref[:, spot].astype(F32) + v.astype(F32)).astype(BF16)
             j += 1
 
 
@@ -318,7 +505,8 @@
         grid_spec=pltpu.PrefetchScalarGridSpec(
             num_scalar_prefetch=1, grid=(n_m,),
             in_specs=[pl.BlockSpec((tm, dim), spot)]
-            + [pl.BlockSpec((tm, t.shape[1]), lambda m, p: (m, 0)) for t in totals]
+            + [pl.BlockSpec((tm, t.shape[1]), lambda m, p: (m, 0)) if t.ndim == 2 else
+               pl.BlockSpec(t.shape[:2] + (tm, t.shape[3]), lambda m, p: (0, 0, m, 0)) for t in totals]
             + [pl.BlockSpec(memory_space=pl.ANY)] * aliased,
             out_specs=pl.BlockSpec((tm, dim), spot)),
         out_shape=jax.ShapeDtypeStruct((rows, dim), BF16),
@@ -388,7 +576,7 @@
         chip, core = me // 2, me % 2
         n_chip = n_wg // 2
         order = []
-        for step in (0, -1, 1, 2):
+        for step in CHIP_STEPS:
             c = (chip + step + n_chip) % n_chip
             order += [2 * c + core, 2 * c + 1 - core]
         idx = jnp.stack(order).astype(jnp.int32)
@@ -441,7 +629,8 @@
                                           (k_cache, v_cache))
         s_b = tie(s_b, q1)
         one_b = ring_one(*s_b)
-        far_a = tie(far_a, *s_b)
+        act1 = attention(after(q1, *s_b), k_cache, v1, valid_row, 1, oc + ff)
+        far_a = tie(far_a, act1)
         p_a = ring_pieces(near_a, sw_near, far_a, swaps(far_a))
         act0 = gate_up(z0, p_a, act0, oc, 0, 3)
 
@@ -470,14 +659,11 @@
         part_b = down(act0, [pair_3], dim - part_a.shape[1], 2, part_b)
         tot_b = lax.psum(after(part_b, tot_a), 'tp')
 
-        act1 = attention(after(q1, part_b), k_cache, v1, valid_row, 1, oc + ff)
-        act1 = gate_up(z1, p_a, act1, oc)
+        act1 = gate_up(z1, p_a, after(act1, part_b), oc)
         act1 = gate_up(z1, p_b, act1, oc + cut_at)
-        part_c = down(act1, [pair_0] + near + [pair_3])
-        tot_c = lax.psum(after(part_c, tot_b), 'tp')
-
-        y = residual(x2, [tot_a, tot_b], idx, None, 0, seq)
-        y = residual(x2, [tot_c], idx, y, 1, seq)
+        y = down_ring(act1, x2, [pair_0] + near + [pair_3])
+
+        y = residual(x2, [tot_a, tot_b], idx, y, 0, seq)
         out3 = lambda v: v.reshape(n_prompts, seq, v.shape[-1])
         return out3(y), out3(k_cache), out3(v_cache)
 

time: 694 us -> 671 us (0.967)
  waiting for transfers between devices: 212 us -> 65.6 us
  Pallas kernels: 402 us -> 510 us
  local copies, waits for them, and re-layouts: 11.5 us -> 25.5 us
    pallas_call x2 -> x3, Pallas kernels: 37.3 us -> 206 us  [the longest x1 176 us: down_ring(): pl.pallas_call(functools.partial(ring_kernel, len(ws)), in_specs=[pl.Bloc...]
    psum x1 -> x0, waiting for transfers between devices: 144 us -> none  [local_step(): tot_c = lax.psum(after(part_c, tot_b), 'tp')]
    pallas_call x4 -> x3, Pallas kernels: 110 us -> 60.5 us  [down(): pl.pallas_call(functools.partial(down_kernel, plan), grid=(len(pairs), se...]
    unnamed x49 -> x50, local copies, waits for them, and re-layouts: 4.49 us -> 18.7 us
    pallas_call x2 -> x1, Pallas kernels: 20.5 us -> 10.2 us  [residual(): pl.pallas_call(functools.partial(add_kernel, len(totals)), grid_spec=pltp...]
  transfers between devices with their start and end apart: 54 -> 53, of which waited for: 16 -> 15; matrix products, arithmetic and copies ran while one was open for 2% -> 3% of each run, Pallas kernels for 57% -> 76%
where the time goes in v2:
time: 671 us; the launch traced here: 660 us
  Pallas kernels  510 us (76%)
  waiting for transfers between devices  65.6 us (10%)
  starting transfers between devices  34.7 us (5%)
  local copies, waits for them, and re-layouts  25.5 us (4%)
  between operations  15 us (2%)
  other arithmetic  9.22 us (1%)
    pallas_call x5, Pallas kernels, gate_up(): pl.pallas_call(gu_kernel, grid=(cols // (2 * FF_TILE), seq // tm), in_spe...  178 us
    pallas_call x1, Pallas kernels, down_ring(): pl.pallas_call(functools.partial(ring_kernel, len(ws)), in_specs=[pl.Bloc...  176 us
    ppermute x51, waiting for transfers between devices, shift(): return lax.ppermute(val, 'wg', pairs)  65.4 us
    pallas_call x3, Pallas kernels, down(): pl.pallas_call(functools.partial(down_kernel, plan), grid=(len(pairs), se...  60.5 us
    ppermute x51, starting transfers between devices, shift(): return lax.ppermute(val, 'wg', pairs)  34.6 us
    pallas_call x2, Pallas kernels, attention(): pl.pallas_call(functools.partial(attn_kernel, n_blk, hd ** (-0.5), hd), g...  29.9 us
    pallas_call x2, Pallas kernels, qkv(): pl.pallas_call(functools.partial(qkv_kernel, n_heads, hd, len(caches)), g...  29.9 us
    pallas_call x2, Pallas kernels, layer_norm(): pl.pallas_call(ln_kernel, grid_spec=pltpu.PrefetchScalarGridSpec(num_scal...  25.4 us
  transfers between devices with their start and end apart: 53, of which 15 were waited for; matrix products, arithmetic and copies ran while one was open for 3% of the time, Pallas kernels for 76%

profile of v2, /device:TPU:97, one launch (start us, length us, event | category | flops | bytes accessed | tf_op | source)
XLA Modules:
  0.0 659.8 jit_solution(9493004937381197748)
XLA Ops:
  17.9 12.8 %ln.2.refs_0_ = bf16[2048,2048]{1,0:T(8,128)(2,1)} custom-call(s32[8]{0:T(128)} %fusion.2.pos_ref, bf16[4096,2048]{1,0:T(8,128)(2,1)} %bitcast.17, f32[1,2048]{1,0:T(1,128)} %bitcast.26), custom_call_target="tpu_custom_call" | custom-call | flops 5000000000 | bytes 16777216 | tf_op jit(solution)/shard_map/ln/pallas_call | solution.py:53
  35.7 4.7 fusion
  42.2 12.7 %ln.3.refs_0_ = bf16[2048,2048]{1,0:T(8,128)(2,1)} custom-call(s32[8]{0:T(128)} %fusion.2.pos_ref, bf16[4096,2048]{1,0:T(8,128)(2,1)} %bitcast.18, f32[1,2048]{1,0:T(1,128)} %bitcast.27), custom_call_target="tpu_custom_call" | custom-call | flops 5000000000 | bytes 16777216 | tf_op jit(solution)/shard_map/ln/pallas_call | solution.py:53
  59.2 3.0 collective-permute-start.7
  62.3 2.6 collective-permute-start.5
  64.9 14.9 %qkv.2 = (bf16[2048,512]{1,0:T(8,128)(2,1)}, bf16[4096,256]{1,0:T(8,128)(2,1)}, bf16[4096,256]{1,0:T(8,128)(2,1)}, bf16[2048,256]{1,0:T(8,128)(2,1)}) custom-call(bf16[2048,2048]{1,0:T(8,128)(2,1)} %ln.2.refs_0_, f32[2048,128]{1,0:T(8,128)} %get-tuple-element.122.refs_1_, f32[2048,128]{1,0:T(8,128)} %get-tuple-element.121.refs_2_, s32[4096,1]{1,0:T(8,128)} %bitcast.22, ...), custom_call_target="tpu_custom_call" | custom-call | flops 8589934592 | bytes 16777216 | tf_op jit(solution)/shard_map/qkv/pallas_call | solution.py:120
  79.9 14.8 %attn.2.refs_33_ = bf16[2048,4608]{1,0:T(8,128)(2,1)} custom-call(bf16[2048,512]{1,0:T(8,128)(2,1)} %get-tuple-element.67.q_ref, bf16[4096,256]{1,0:T(8,128)(2,1)} %get-tuple-element.68.k_ref.refs_14_, bf16[2048,256]{1,0:T(8,128)(2,1)} %get-tuple-element.69.v_ref, s32[2,1,2048]{2,1,0:T(1,128)} %reshape.36.valid_ref), custom_call_target="tpu_custom_call" | custom-call | flops 16000000000 | bytes 6291456 | tf_op jit(solution)/shard_map/attn/pallas_call | solution.py:179
  94.7 26.5 %collective-permute-done.6.refs_6_.refs_22_ = bf16[128,5120]{1,0:T(8,128)(2,1)} collective-permute-done((bf16[128,5120]{1,0:T(8,128)(2,1)S(1)}, bf16[128,5120]{1,0:T(8,128)(2,1)}, u32[]{:S(2)}, u32[]{:S(2)}) %collective-permute-start.6) | collective-permute-done | bytes 1310752 | tf_op jit(solution)/shard_map/ppermute | solution.py:540
  123.3 2.7 collective-permute-start.24
  125.9 15.0 %qkv.3 = (bf16[2048,512]{1,0:T(8,128)(2,1)}, bf16[4096,256]{1,0:T(8,128)(2,1)}, bf16[4096,256]{1,0:T(8,128)(2,1)}, bf16[2048,256]{1,0:T(8,128)(2,1)}) custom-call(bf16[2048,2048]{1,0:T(8,128)(2,1)} %ln.3.refs_0_, f32[2048,128]{1,0:T(8,128)} %get-tuple-element.122.refs_1_, ...), custom_call_target="tpu_custom_call", output_to_operand_aliasing={{1}: (14, {}), {2}: (15, {})} | custom-call | flops 8589934592 | bytes 16777216 | tf_op jit(solution)/shard_map/qkv/pallas_call | solution.py:120
  141.0 15.1 %attn.3.refs_33_ = bf16[2048,4608]{1,0:T(8,128)(2,1)} custom-call(bf16[2048,512]{1,0:T(8,128)(2,1)} %get-tuple-element.81.q_ref, bf16[4096,256]{1,0:T(8,128)(2,1)} %get-tuple-element.82.k_ref, bf16[2048,256]{1,0:T(8,128)(2,1)} %get-tuple-element.83.v_ref, s32[2,1,2048]{2,1,0:T(1,128)} %reshape.36.valid_ref), custom_call_target="tpu_custom_call" | custom-call | flops 16000000000 | bytes 6291456 | tf_op jit(solution)/shard_map/attn/pallas_call | solution.py:179
  167.3 33.5 %gate_up.5.refs_33_ = bf16[2048,4608]{1,0:T(8,128)(2,1)} custom-call(bf16[2048,2048]{1,0:T(8,128)(2,1)} %ln.2.refs_0_, bf16[128,5120]{1,0:T(8,128)(2,1)} %copy-done.1, bf16[128,5120]{1,0:T(8,128)(2,1)} %copy-done, bf16[128,5120]{1,0:T(8,128)(2,1)} %collective-permute-done.17.refs_3_.refs_19_, ...), custom_call_target="tpu_custom_call", output_to_operand_aliasing={{}: (33, {})} | custom-call | flops 25769803776 | bytes 16777216 | tf_op jit(solution)/shard_map/gate_up/pallas_call | solution.py:222
  204.0 17.2 %collective-permute-done.33.refs_13_.refs_29_ = bf16[128,3072]{1,0:T(8,128)(2,1)} collective-permute-done((bf16[128,3072]{1,0:T(8,128)(2,1)}, bf16[128,3072]{1,0:T(8,128)(2,1)}, u32[]{:S(2)}, u32[]{:S(2)}) %collective-permute-start.33) | collective-permute-done | bytes 786464 | tf_op jit(solution)/shard_map/ppermute | solution.py:540
  221.3 24.0 %gate_up.6.refs_33_ = bf16[2048,4608]{1,0:T(8,128)(2,1)} custom-call(bf16[2048,2048]{1,0:T(8,128)(2,1)} %ln.2.refs_0_, bf16[128,5120]{1,0:T(8,128)(2,1)} %copy-done.1, bf16[128,5120]{1,0:T(8,128)(2,1)} %copy-done, bf16[128,5120]{1,0:T(8,128)(2,1)} %collective-permute-done.17.refs_3_.refs_19_, ...), custom_call_target="tpu_custom_call", output_to_operand_aliasing={{}: (33, {})} | custom-call | flops 17179869184 | bytes 16777216 | tf_op jit(solution)/shard_map/gate_up/pallas_call | solution.py:222
  247.6 2.6 collective-permute-done.29.refs_7_.refs_23_
  257.9 33.5 %gate_up.7.act_ref = bf16[2048,4608]{1,0:T(8,128)(2,1)} custom-call(bf16[2048,2048]{1,0:T(8,128)(2,1)} %ln.2.refs_0_, bf16[128,3072]{1,0:T(8,128)(2,1)} %pad_maximum_fusion.3.refs_1_.refs_17_, bf16[128,3072]{1,0:T(8,128)(2,1)} %pad_maximum_fusion.4.refs_2_.refs_18_, bf16[128,3072]{1,0:T(8,128)(2,1)} %copy-done.16, ...), custom_call_target="tpu_custom_call", output_to_operand_aliasing={{}: (33, {})} | custom-call | flops 25769803776 | bytes 16777216 | tf_op jit(solution)/shard_map/gate_up/pallas_call | solution.py:222
  291.4 16.6 %down.3 = bf16[2048,512]{1,0:T(8,128)(2,1)} custom-call(bf16[2048,4608]{1,0:T(8,128)(2,1)} %gate_up.7.act_ref, bf16[2304,256]{1,0:T(8,128)(2,1)} %copy-done.10, bf16[2304,256]{1,0:T(8,128)(2,1)} %copy-done.9, bf16[2304,256]{1,0:T(8,128)(2,1)} %copy-done.14, bf16[2304,256]{1,0:T(8,128)(2,1)} %collective-permute-done.38.refs_3_.refs_5_), custom_call_target="tpu_custom_call" | custom-call | flops 9663676416 | bytes 18874368 | tf_op jit(solution)/shard_map/down/pallas_call | solution.py:287
  316.4 27.2 %down.4.refs_4_ = bf16[2048,1536]{1,0:T(8,128)(2,1)} custom-call(bf16[2048,4608]{1,0:T(8,128)(2,1)} %gate_up.7.act_ref, bf16[2304,256]{1,0:T(8,128)(2,1)} %collective-permute-done.39.refs_0_.refs_6_, bf16[2304,256]{1,0:T(8,128)(2,1)} %collective-permute-done.41.refs_1_.refs_7_, bf16[2304,256]{1,0:T(8,128)(2,1)} %collective-permute-done.45.refs_2_.refs_8_, ...), custom_call_target="tpu_custom_call" | custom-call | flops 19327352832 | bytes 18874368 | tf_op jit(solution)/shard_map/down/pallas_call | solution.py:287
  348.5 16.7 %down.5 = bf16[2048,1536]{1,0:T(8,128)(2,1)} custom-call(bf16[2048,4608]{1,0:T(8,128)(2,1)} %gate_up.7.act_ref, bf16[2304,256]{1,0:T(8,128)(2,1)} %copy-done.5, bf16[2304,256]{1,0:T(8,128)(2,1)} %copy-done.6, bf16[2304,256]{1,0:T(8,128)(2,1)} %copy-done.7, ...), custom_call_target="tpu_custom_call", output_to_operand_aliasing={{}: (5, {})} | custom-call | flops 9663676416 | bytes 18874368 | tf_op jit(solution)/shard_map/down/pallas_call | solution.py:287
  365.3 53.0 %gate_up.8.refs_33_ = bf16[2048,4608]{1,0:T(8,128)(2,1)} custom-call(bf16[2048,2048]{1,0:T(8,128)(2,1)} %ln.3.refs_0_, bf16[128,5120]{1,0:T(8,128)(2,1)} %copy-done.1, bf16[128,5120]{1,0:T(8,128)(2,1)} %copy-done, bf16[128,5120]{1,0:T(8,128)(2,1)} %collective-permute-done.17.refs_3_.refs_19_, ...), custom_call_target="tpu_custom_call", output_to_operand_aliasing={{}: (33, {})} | custom-call | flops 42949672960 | bytes 16777216 | tf_op jit(solution)/shard_map/gate_up/pallas_call | solution.py:222
  418.3 33.7 %gate_up.9.refs_0_ = bf16[2048,4608]{1,0:T(8,128)(2,1)} custom-call(bf16[2048,2048]{1,0:T(8,128)(2,1)} %ln.3.refs_0_, bf16[128,3072]{1,0:T(8,128)(2,1)} %pad_maximum_fusion.3.refs_1_.refs_17_, bf16[128,3072]{1,0:T(8,128)(2,1)} %pad_maximum_fusion.4.refs_2_.refs_18_, bf16[128,3072]{1,0:T(8,128)(2,1)} %copy-done.16, ...), custom_call_target="tpu_custom_call", output_to_operand_aliasing={{}: (33, {})} | custom-call | flops 25769803776 | bytes 16777216 | tf_op jit(solution)/shard_map/gate_up/pallas_call | solution.py:222
  452.0 176.2 %down_ring.1.refs_2_ = bf16[4096,2048]{1,0:T(8,128)(2,1)} custom-call(bf16[2048,4608]{1,0:T(8,128)(2,1)} %gate_up.9.refs_0_, bf16[4096,2048]{1,0:T(8,128)(2,1)} %bitcast.19, bf16[2304,256]{1,0:T(8,128)(2,1)} %copy-done.10, bf16[2304,256]{1,0:T(8,128)(2,1)} %copy-done.9, bf16[2304,256]{1,0:T(8,128)(2,1)} %copy-done.14, ...), custom_call_target="tpu_custom_call" | custom-call | flops 140000002048 | bytes 18874368 | tf_op jit(solution)/shard_map/down_ring/pallas_call | solution.py:465
  628.2 10.2 %residual.1 = bf16[4096,2048]{1,0:T(8,128)(2,1)} custom-call(s32[8]{0:T(128)} %stack.35.idx_ref, bf16[4096,2048]{1,0:T(8,128)(2,1)} %bitcast.20, bf16[2048,512]{1,0:T(8,128)(2,1)} %all-reduce.3.cloned.1.call-done.refs_0_, bf16[2048,1536]{1,0:T(8,128)(2,1)} %all-reduce.5.cloned.1.call-done.refs_1_, ...), custom_call_target="tpu_custom_call", output_to_operand_aliasing={{}: (4, {})} | custom-call | flops 5000000000 | bytes 25165824 | tf_op jit(solution)/shard_map/residual/pallas_call | solution.py:503
  638.4 14.2 %copy.38 = bf16[2,2048,2048]{2,1,0:T(8,128)(2,1)} copy(bf16[2,2048,2048]{2,1,0:T(8,128)(2,1)} %bitcast.21) | data formatting | bytes 33554432
  (165 shorter events, 61.5 us)
Async XLA Ops:
  7.2 358.0 %all-reduce.3.cloned.1.call-start = ((), (), s32[]{:S(2)}) async-start(), calls=%async_computation | async-start | bytes 4194304 | tf_op jit(solution)/shard_map/psum | solution.py:650
  9.2 50.0 %collective-permute-start.8 = (bf16[256,1024]{1,0:T(8,128)(2,1)S(1)}, bf16[256,1024]{1,0:T(8,128)(2,1)}, u32[]{:S(2)}, u32[]{:S(2)}) collective-permute-start(bf16[256,1024]{1,0:T(8,128)(2,1)S(1)} %constant_dynamic-update-slice_fusion.refs_4_), channel_id=1, source_target_pairs={{0,1},{1,0},{2,3},{3,2},{4,5},{5,4},{6,7},{7,6},{8,9},{9,8},{10,11... | collective-permute-start | bytes 1572872 | tf_op jit(solution)/shard_map/ppermute | solution.py:540
  59.2 35.5 %collective-permute-start.7 = (bf16[128,5120]{1,0:T(8,128)(2,1)S(1)}, bf16[128,5120]{1,0:T(8,128)(2,1)}, u32[]{:S(2)}, u32[]{:S(2)}) collective-permute-start(bf16[128,5120]{1,0:T(8,128)(2,1)S(1)} %pad_maximum_fusion.refs_1_.refs_17_), channel_id=1, source_target_pairs={{0,6},{1,7},{2,0},{3,1},{4,2},{5,3},{6,4},{7,5},{8,14},{9,15},{10,... | collective-permute-start | bytes 3932168 | tf_op jit(solution)/shard_map/ppermute | solution.py:540
  62.2 59.1 %collective-permute-start.6 = (bf16[128,5120]{1,0:T(8,128)(2,1)S(1)}, bf16[128,5120]{1,0:T(8,128)(2,1)}, u32[]{:S(2)}, u32[]{:S(2)}) collective-permute-start(bf16[128,5120]{1,0:T(8,128)(2,1)S(1)} %pad_maximum_fusion.1.refs_2_.refs_18_), channel_id=1, source_target_pairs={{0,2},{1,3},{2,4},{3,5},{4,6},{5,7},{6,0},{7,1},{8,10},{9,11},{10,... | collective-permute-start | bytes 3932168 | tf_op jit(solution)/shard_map/ppermute | solution.py:540
  62.3 58.9 %collective-permute-start.5 = (bf16[128,5120]{1,0:T(8,128)(2,1)S(1)}, bf16[128,5120]{1,0:T(8,128)(2,1)}, u32[]{:S(2)}, u32[]{:S(2)}) collective-permute-start(bf16[128,5120]{1,0:T(8,128)(2,1)S(1)} %pad_maximum_fusion.1.refs_2_.refs_18_), channel_id=1, source_target_pairs={{0,6},{1,7},{2,0},{3,1},{4,2},{5,3},{6,4},{7,5},{8,14},{9,15},{10,... | collective-permute-start | bytes 3932168 | tf_op jit(solution)/shard_map/ppermute | solution.py:540
  121.2 35.7 %collective-permute-start.17 = (bf16[128,5120]{1,0:T(8,128)(2,1)S(1)}, bf16[128,5120]{1,0:T(8,128)(2,1)}, u32[]{:S(2)}, u32[]{:S(2)}) collective-permute-start(bf16[128,5120]{1,0:T(8,128)(2,1)S(1)} %pad_maximum_fusion.refs_1_.refs_17_), channel_id=1, source_target_pairs={{0,1},{1,0},{2,3},{3,2},{4,5},{5,4},{6,7},{7,6},{8,9},{9,8},{10,11... | collective-permute-start | bytes 3932168 | tf_op jit(solution)/shard_map/ppermute | solution.py:540
  122.8 34.6 %collective-permute-start.18 = (bf16[128,5120]{1,0:T(8,128)(2,1)S(1)}, bf16[128,5120]{1,0:T(8,128)(2,1)}, u32[]{:S(2)}, u32[]{:S(2)}) collective-permute-start(bf16[128,5120]{1,0:T(8,128)(2,1)S(1)} %pad_maximum_fusion.1.refs_2_.refs_18_), channel_id=1, source_target_pairs={{0,1},{1,0},{2,3},{3,2},{4,5},{5,4},{6,7},{7,6},{8,9},{9,8},{10,11... | collective-permute-start | bytes 3932168 | tf_op jit(solution)/shard_map/ppermute | solution.py:540
  122.9 34.6 %collective-permute-start.20 = (bf16[128,5120]{1,0:T(8,128)(2,1)}, bf16[128,5120]{1,0:T(8,128)(2,1)}, u32[]{:S(2)}, u32[]{:S(2)}) collective-permute-start(bf16[128,5120]{1,0:T(8,128)(2,1)} %collective-permute-done.6.refs_6_.refs_22_), channel_id=1, source_target_pairs={{0,1},{1,0},{2,3},{3,2},{4,5},{5,4},{6,7},{7,6},{8,9},{9,8},{10,11... | collective-permute-start | bytes 3932168 | tf_op jit(solution)/shard_map/ppermute | solution.py:540
  123.3 33.6 %collective-permute-start.24 = (bf16[128,5120]{1,0:T(8,128)(2,1)}, bf16[128,5120]{1,0:T(8,128)(2,1)}, u32[]{:S(2)}, u32[]{:S(2)}) collective-permute-start(bf16[128,5120]{1,0:T(8,128)(2,1)} %collective-permute-done.5.refs_10_.refs_26_), channel_id=1, source_target_pairs={{0,6},{1,7},{2,0},{3,1},{4,2},{5,3},{6,4},{7,5},{8,14},{9,15},{10,... | collective-permute-start | bytes 3932168 | tf_op jit(solution)/shard_map/ppermute | solution.py:540
  159.8 41.0 %collective-permute-start.16 = (bf16[128,3072]{1,0:T(8,128)(2,1)}, bf16[128,3072]{1,0:T(8,128)(2,1)}, u32[]{:S(2)}, u32[]{:S(2)}) collective-permute-start(bf16[128,3072]{1,0:T(8,128)(2,1)} %pad_maximum_fusion.3.refs_1_.refs_17_), channel_id=1, source_target_pairs={{0,6},{1,7},{2,0},{3,1},{4,2},{5,3},{6,4},{7,5},{8,14},{9,15},{10,... | collective-permute-start | bytes 2359304 | tf_op jit(solution)/shard_map/ppermute | solution.py:540
  161.7 39.2 %collective-permute-start.13 = (bf16[128,3072]{1,0:T(8,128)(2,1)}, bf16[128,3072]{1,0:T(8,128)(2,1)}, u32[]{:S(2)}, u32[]{:S(2)}) collective-permute-start(bf16[128,3072]{1,0:T(8,128)(2,1)} %pad_maximum_fusion.3.refs_1_.refs_17_), channel_id=1, source_target_pairs={{0,2},{1,3},{2,4},{3,5},{4,6},{5,7},{6,0},{7,1},{8,10},{9,11},{10,... | collective-permute-start | bytes 2359304 | tf_op jit(solution)/shard_map/ppermute | solution.py:540
  163.5 37.4 %collective-permute-start.15 = (bf16[128,3072]{1,0:T(8,128)(2,1)S(1)}, bf16[128,3072]{1,0:T(8,128)(2,1)}, u32[]{:S(2)}, u32[]{:S(2)}) collective-permute-start(bf16[128,3072]{1,0:T(8,128)(2,1)S(1)} %copy-done.11), channel_id=1, source_target_pairs={{0,2},{1,3},{2,4},{3,5},{4,6},{5,7},{6,0},{7,1},{8,10},{9,11},{10,... | collective-permute-start | bytes 2359304 | tf_op jit(solution)/shard_map/ppermute | solution.py:540
  165.3 35.6 %collective-permute-start.14 = (bf16[128,3072]{1,0:T(8,128)(2,1)S(1)}, bf16[128,3072]{1,0:T(8,128)(2,1)}, u32[]{:S(2)}, u32[]{:S(2)}) collective-permute-start(bf16[128,3072]{1,0:T(8,128)(2,1)S(1)} %copy-done.11), channel_id=1, source_target_pairs={{0,6},{1,7},{2,0},{3,1},{4,2},{5,3},{6,4},{7,5},{8,14},{9,15},{10,... | collective-permute-start | bytes 2359304 | tf_op jit(solution)/shard_map/ppermute | solution.py:540
  202.7 43.9 %collective-permute-start.27 = (bf16[128,3072]{1,0:T(8,128)(2,1)}, bf16[128,3072]{1,0:T(8,128)(2,1)S(1)}, u32[]{:S(2)}, u32[]{:S(2)}) collective-permute-start(bf16[128,3072]{1,0:T(8,128)(2,1)} %pad_maximum_fusion.3.refs_1_.refs_17_), channel_id=1, source_target_pairs={{0,1},{1,0},{2,3},{3,2},{4,5},{5,4},{6,7},{7,6},{8,9},{9,8},{10,11... | collective-permute-start | bytes 2359304 | tf_op jit(solution)/shard_map/ppermute | solution.py:540
  203.4 43.4 %collective-permute-start.28 = (bf16[128,3072]{1,0:T(8,128)(2,1)S(1)}, bf16[128,3072]{1,0:T(8,128)(2,1)}, u32[]{:S(2)}, u32[]{:S(2)}) collective-permute-start(bf16[128,3072]{1,0:T(8,128)(2,1)S(1)} %copy-done.11), channel_id=1, source_target_pairs={{0,1},{1,0},{2,3},{3,2},{4,5},{5,4},{6,7},{7,6},{8,9},{9,8},{10,11... | collective-permute-start | bytes 2359304 | tf_op jit(solution)/shard_map/ppermute | solution.py:540
  203.5 43.6 %collective-permute-start.30 = (bf16[128,3072]{1,0:T(8,128)(2,1)}, bf16[128,3072]{1,0:T(8,128)(2,1)}, u32[]{:S(2)}, u32[]{:S(2)}) collective-permute-start(bf16[128,3072]{1,0:T(8,128)(2,1)} %collective-permute-done.15.refs_6_.refs_22_), channel_id=1, source_target_pairs={{0,1},{1,0},{2,3},{3,2},{4,5},{5,4},{6,7},{7,6},{8,9},{9,8},{10,11... | collective-permute-start | bytes 2359304 | tf_op jit(solution)/shard_map/ppermute | solution.py:540
  203.9 43.4 %collective-permute-start.31 = (bf16[128,3072]{1,0:T(8,128)(2,1)}, bf16[128,3072]{1,0:T(8,128)(2,1)}, u32[]{:S(2)}, u32[]{:S(2)}) collective-permute-start(bf16[128,3072]{1,0:T(8,128)(2,1)} %collective-permute-done.16.refs_9_.refs_25_), channel_id=1, source_target_pairs={{0,1},{1,0},{2,3},{3,2},{4,5},{5,4},{6,7},{7,6},{8,9},{9,8},{10,11... | collective-permute-start | bytes 2359304 | tf_op jit(solution)/shard_map/ppermute | solution.py:540
  250.2 57.8 %collective-permute-start.42 = (bf16[2304,256]{1,0:T(8,128)(2,1)S(1)}, bf16[2304,256]{1,0:T(8,128)(2,1)}, u32[]{:S(2)}, u32[]{:S(2)}) collective-permute-start(bf16[2304,256]{1,0:T(8,128)(2,1)S(1)} %get-tuple-element.97.refs_0_.refs_2_), channel_id=1, source_target_pairs={{0,6},{1,7},{2,0},{3,1},{4,2},{5,3},{6,4},{7,5},{8,14},{9,15},{10,... | collective-permute-start | bytes 3538952 | tf_op jit(solution)/shard_map/ppermute | solution.py:540
  251.3 56.7 %collective-permute-start.39 = (bf16[2304,256]{1,0:T(8,128)(2,1)S(1)}, bf16[2304,256]{1,0:T(8,128)(2,1)}, u32[]{:S(2)}, u32[]{:S(2)}) collective-permute-start(bf16[2304,256]{1,0:T(8,128)(2,1)S(1)} %get-tuple-element.97.refs_0_.refs_2_), channel_id=1, source_target_pairs={{0,2},{1,3},{2,4},{3,5},{4,6},{5,7},{6,0},{7,1},{8,10},{9,11},{10,... | collective-permute-start | bytes 3538952 | tf_op jit(solution)/shard_map/ppermute | solution.py:540
  253.1 55.0 %collective-permute-start.41 = (bf16[2304,256]{1,0:T(8,128)(2,1)S(1)}, bf16[2304,256]{1,0:T(8,128)(2,1)}, u32[]{:S(2)}, u32[]{:S(2)}) collective-permute-start(bf16[2304,256]{1,0:T(8,128)(2,1)S(1)} %get-tuple-element.98.refs_1_.refs_3_), channel_id=1, source_target_pairs={{0,2},{1,3},{2,4},{3,5},{4,6},{5,7},{6,0},{7,1},{8,10},{9,11},{10,... | collective-permute-start | bytes 3538952 | tf_op jit(solution)/shard_map/ppermute | solution.py:540
  253.5 54.5 %collective-permute-start.40 = (bf16[2304,256]{1,0:T(8,128)(2,1)S(1)}, bf16[2304,256]{1,0:T(8,128)(2,1)}, u32[]{:S(2)}, u32[]{:S(2)}) collective-permute-start(bf16[2304,256]{1,0:T(8,128)(2,1)S(1)} %get-tuple-element.98.refs_1_.refs_3_), channel_id=1, source_target_pairs={{0,6},{1,7},{2,0},{3,1},{4,2},{5,3},{6,4},{7,5},{8,14},{9,15},{10,... | collective-permute-start | bytes 3538952 | tf_op jit(solution)/shard_map/ppermute | solution.py:540
  256.7 34.7 %collective-permute-start.38 = (bf16[2304,256]{1,0:T(8,128)(2,1)S(1)}, bf16[2304,256]{1,0:T(8,128)(2,1)}, u32[]{:S(2)}, u32[]{:S(2)}) collective-permute-start(bf16[2304,256]{1,0:T(8,128)(2,1)S(1)} %get-tuple-element.98.refs_1_.refs_3_), channel_id=1, source_target_pairs={{0,1},{1,0},{2,3},{3,2},{4,5},{5,4},{6,7},{7,6},{8,9},{9,8},{10,11... | collective-permute-start | bytes 3538952 | tf_op jit(solution)/shard_map/ppermute | solution.py:540
  309.2 319.0 %all-reduce.5.cloned.1.call-start = ((), (), s32[]{:S(2)}) async-start(), calls=%async_computation.1 | async-start | bytes 12582912 | tf_op jit(solution)/shard_map/psum | solution.py:660
  309.3 34.3 %collective-permute-start.43 = (bf16[2304,256]{1,0:T(8,128)(2,1)}, bf16[2304,256]{1,0:T(8,128)(2,1)S(1)}, u32[]{:S(2)}, u32[]{:S(2)}) collective-permute-start(bf16[2304,256]{1,0:T(8,128)(2,1)} %collective-permute-done.39.refs_0_.refs_6_), channel_id=1, source_target_pairs={{0,2},{1,3},{2,4},{3,5},{4,6},{5,7},{6,0},{7,1},{8,10},{9,11},{10,... | collective-permute-start | bytes 3538952 | tf_op jit(solution)/shard_map/ppermute | solution.py:540
  (52 other events, 868.1 us)
Sparse Core Ops, SparseCore 0:
  309.4 53.6 all-reduce.2
  366.1 127.6 all-reduce.4

commit v3 on v2

--- a/solution.py
+++ b/solution.py
@@ -357,7 +357,7 @@
     def out_copy(t, side, k):
         q, h, row, col = place(t, side, k)
         src = act_s.at[h, pl.ds(pl.multiple_of(row, quarter), quarter), pl.ds(col, blk)]
-        dst = y_ref.at[pl.ds(pl.multiple_of(y_ref.shape[0] - seq + q * quarter, quarter), quarter), pl.ds(col, blk)]
+        dst = y_ref.at[pl.ds(pl.multiple_of(q * quarter, quarter), quarter), pl.ds(col, blk)]
         return pltpu.make_async_copy(src, dst, out_sem.at[t, side, k])
 
     def finish(t, side, k):
@@ -435,9 +435,9 @@
 
     lax.fori_loop(0, n_pairs, pair, 0)
     for i in range(2):
-        x_copy(i, y_ref.shape[0] - seq).start()
+        x_copy(i, x_ref.shape[0] - seq).start()
     for i in range(2):
-        x_copy(i, y_ref.shape[0] - seq).wait()
+        x_copy(i, x_ref.shape[0] - seq).wait()
 
     state = [3] * (n_pairs - 1) + [1]
     while min(state) <= n_steps:
@@ -466,7 +466,7 @@
         functools.partial(ring_kernel, len(ws)),
         in_specs=[pl.BlockSpec(memory_space=pl.ANY)] * (2 + len(ws)),
         out_specs=pl.BlockSpec(memory_space=pl.ANY),
-        out_shape=jax.ShapeDtypeStruct(x.shape, BF16),
+        out_shape=jax.ShapeDtypeStruct((seq, x.shape[1]), BF16),
         scratch_shapes=[pltpu.VMEM((2, seq // 2, kdim), BF16), pltpu.VMEM((2, kdim, 2 * blk), BF16),
                         pltpu.VMEM(shape, BF16), pltpu.VMEM((n_pairs, 2, n_tp - 1, seq // n_tp, blk), BF16),
                         pltpu.VMEM(shape, BF16),
@@ -479,42 +479,43 @@
     )(act, x, *ws)
 
 
-def add_kernel(n_tot, idx_ref, x_ref, *refs):
-    tots, y_ref = refs[:n_tot], refs[-1]
+def add_kernel(n_m, idx_ref, x_ref, *refs):
+    tots, last_ref, y_ref = refs[:-2], refs[-2], refs[-1]
     blk = x_ref.shape[1] // N_PIECES
-    j = 0
-    for t in tots:
-        if len(t.shape) == 4:
-            parts = [t[i, side] for i in range(t.shape[0]) for side in range(2)]
-        else:
-            parts = [t[:, c:c + blk] for c in range(0, t.shape[1], blk)]
-        for v in parts:
-            spot = pl.ds(pl.multiple_of(idx_ref[j] * blk, blk), blk)
-            y_ref[:, spot] = (x_ref[:, spot].astype(F32) + v.astype(F32)).astype(BF16)
-            j += 1
-
-
-def residual(x, totals, idx, y, prompt, seq):
+
+    @pl.when(pl.program_id(0) < n_m)
+    def _():
+        j = 0
+        for t in tots:
+            for c in range(0, t.shape[1], blk):
+                spot = pl.ds(pl.multiple_of(idx_ref[j] * blk, blk), blk)
+                y_ref[:, spot] = (x_ref[:, spot].astype(F32) + t[:, c:c + blk].astype(F32)).astype(BF16)
+                j += 1
+
+    @pl.when(pl.program_id(0) >= n_m)
+    def _():
+        y_ref[...] = last_ref[...]
+
+
+def residual(x, totals, idx, last):
     rows, dim = x.shape
+    seq = last.shape[0]
     tm = 512
     n_m = seq // tm
-    aliased = 0 if y is None else 1
-    spot = lambda m, p: (prompt * n_m + m, 0)
+    first = lambda m, p: (jnp.minimum(m, n_m - 1), 0)
     return pl.pallas_call(
-        functools.partial(add_kernel, len(totals)),
+        functools.partial(add_kernel, n_m),
         grid_spec=pltpu.PrefetchScalarGridSpec(
-            num_scalar_prefetch=1, grid=(n_m,),
-            in_specs=[pl.BlockSpec((tm, dim), spot)]
-            + [pl.BlockSpec((tm, t.shape[1]), lambda m, p: (m, 0)) if t.ndim == 2 else
-               pl.BlockSpec(t.shape[:2] + (tm, t.shape[3]), lambda m, p: (0, 0, m, 0)) for t in totals]
-            + [pl.BlockSpec(memory_space=pl.ANY)] * aliased,
-            out_specs=pl.BlockSpec((tm, dim), spot)),
+            num_scalar_prefetch=1, grid=(rows // tm,),
+            in_specs=[pl.BlockSpec((tm, dim), first)]
+            + [pl.BlockSpec((tm, t.shape[1]), first) for t in totals]
+            + [pl.BlockSpec((tm, dim), lambda m, p: (jnp.maximum(m - n_m, 0), 0))],
+            out_specs=pl.BlockSpec((tm, dim), lambda m, p: (m, 0))),
         out_shape=jax.ShapeDtypeStruct((rows, dim), BF16),
-        input_output_aliases={2 + len(totals): 0} if aliased else {},
         compiler_params=params(("arbitrary",)),
-        cost_estimate=cost(5e9, seq * dim * 6),
+        cost_estimate=cost(5e9, rows * dim * 6),
         name="residual",
-    )(idx, x, *totals, *([y] if aliased else []))
+    )(idx, x, *totals, last)
 
 
 def rope_tables(seq_len, head_dim):
@@ -661,9 +662,9 @@
 
         act1 = gate_up(z1, p_a, after(act1, part_b), oc)
         act1 = gate_up(z1, p_b, act1, oc + cut_at)
-        y = down_ring(act1, x2, [pair_0] + near + [pair_3])
-
-        y = residual(x2, [tot_a, tot_b], idx, y, 0, seq)
+        y_last = down_ring(act1, x2, [pair_0] + near + [pair_3])
+
+        y = residual(x2, [tot_a, tot_b], idx, y_last)
         out3 = lambda v: v.reshape(n_prompts, seq, v.shape[-1])
         return out3(y), out3(k_cache), out3(v_cache)
 

time: 671 us -> 664 us (0.990)
  local copies, waits for them, and re-layouts: 25.5 us -> 11.5 us
  Pallas kernels: 510 us -> 517 us
    unnamed x50 -> x49, local copies, waits for them, and re-layouts: 18.7 us -> 4.48 us
    pallas_call x1, Pallas kernels: 10.2 us -> 17.4 us  [residual(): pl.pallas_call(functools.partial(add_kernel, n_m), grid_spec=pltpu.Prefet...]
  transfers between devices with their start and end apart: 53 -> 53, of which waited for: 15 -> 15; matrix products, arithmetic and copies ran while one was open for 3% -> 3% of each run, Pallas kernels for 76% -> 77%
where the time goes in v3:
time: 664 us; the launch traced here: 653 us
  Pallas kernels  517 us (78%)
  waiting for transfers between devices  65.5 us (10%)
  starting transfers between devices  34.7 us (5%)
  between operations  15 us (2%)
  local copies, waits for them, and re-layouts  11.5 us (2%)
  other arithmetic  9.23 us (1%)
    pallas_call x5, Pallas kernels, gate_up(): pl.pallas_call(gu_kernel, grid=(cols // (2 * FF_TILE), seq // tm), in_spe...  177 us
    pallas_call x1, Pallas kernels, down_ring(): pl.pallas_call(functools.partial(ring_kernel, len(ws)), in_specs=[pl.Bloc...  176 us
    ppermute x51, waiting for transfers between devices, shift(): return lax.ppermute(val, 'wg', pairs)  65.3 us
    pallas_call x3, Pallas kernels, down(): pl.pallas_call(functools.partial(down_kernel, plan), grid=(len(pairs), se...  60.6 us
    ppermute x51, starting transfers between devices, shift(): return lax.ppermute(val, 'wg', pairs)  34.5 us
    pallas_call x2, Pallas kernels, attention(): pl.pallas_call(functools.partial(attn_kernel, n_blk, hd ** (-0.5), hd), g...  30 us
    pallas_call x2, Pallas kernels, qkv(): pl.pallas_call(functools.partial(qkv_kernel, n_heads, hd, len(caches)), g...  29.9 us
    pallas_call x2, Pallas kernels, layer_norm(): pl.pallas_call(ln_kernel, grid_spec=pltpu.PrefetchScalarGridSpec(num_scal...  25.5 us
  transfers between devices with their start and end apart: 53, of which 15 were waited for; matrix products, arithmetic and copies ran while one was open for 3% of the time, Pallas kernels for 77%

profile of v3, /device:TPU:97, one launch (start us, length us, event | category | flops | bytes accessed | tf_op | source)
XLA Modules:
  0.0 652.7 jit_solution(2747168118259491074)
XLA Ops:
  11.3 2.3 collective-permute-start.1
  17.9 12.8 %ln.2.refs_0_ = bf16[2048,2048]{1,0:T(8,128)(2,1)} custom-call(s32[8]{0:T(128)} %fusion.2.pos_ref, bf16[4096,2048]{1,0:T(8,128)(2,1)} %bitcast.17, f32[1,2048]{1,0:T(1,128)} %bitcast.26), custom_call_target="tpu_custom_call" | custom-call | flops 5000000000 | bytes 16777216 | tf_op jit(solution)/shard_map/ln/pallas_call | solution.py:53
  35.8 4.7 fusion
  42.3 12.7 %ln.3.refs_0_ = bf16[2048,2048]{1,0:T(8,128)(2,1)} custom-call(s32[8]{0:T(128)} %fusion.2.pos_ref, bf16[4096,2048]{1,0:T(8,128)(2,1)} %bitcast.18, f32[1,2048]{1,0:T(1,128)} %bitcast.27), custom_call_target="tpu_custom_call" | custom-call | flops 5000000000 | bytes 16777216 | tf_op jit(solution)/shard_map/ln/pallas_call | solution.py:53
  59.4 3.0 collective-permute-start.7
  62.5 2.6 collective-permute-start.5
  65.1 14.9 %qkv.2 = (bf16[2048,512]{1,0:T(8,128)(2,1)}, bf16[4096,256]{1,0:T(8,128)(2,1)}, bf16[4096,256]{1,0:T(8,128)(2,1)}, bf16[2048,256]{1,0:T(8,128)(2,1)}) custom-call(bf16[2048,2048]{1,0:T(8,128)(2,1)} %ln.2.refs_0_, f32[2048,128]{1,0:T(8,128)} %get-tuple-element.122.refs_1_, f32[2048,128]{1,0:T(8,128)} %get-tuple-element.121.refs_2_, s32[4096,1]{1,0:T(8,128)} %bitcast.22, ...), custom_call_target="tpu_custom_call" | custom-call | flops 8589934592 | bytes 16777216 | tf_op jit(solution)/shard_map/qkv/pallas_call | solution.py:120
  80.0 14.9 %attn.2.refs_33_ = bf16[2048,4608]{1,0:T(8,128)(2,1)} custom-call(bf16[2048,512]{1,0:T(8,128)(2,1)} %get-tuple-element.67.q_ref, bf16[4096,256]{1,0:T(8,128)(2,1)} %get-tuple-element.68.k_ref.refs_14_, bf16[2048,256]{1,0:T(8,128)(2,1)} %get-tuple-element.69.v_ref, s32[2,1,2048]{2,1,0:T(1,128)} %reshape.36.valid_ref), custom_call_target="tpu_custom_call" | custom-call | flops 16000000000 | bytes 6291456 | tf_op jit(solution)/shard_map/attn/pallas_call | solution.py:179
  94.9 26.5 %collective-permute-done.6.refs_6_.refs_22_ = bf16[128,5120]{1,0:T(8,128)(2,1)} collective-permute-done((bf16[128,5120]{1,0:T(8,128)(2,1)S(1)}, bf16[128,5120]{1,0:T(8,128)(2,1)}, u32[]{:S(2)}, u32[]{:S(2)}) %collective-permute-start.6) | collective-permute-done | bytes 1310752 | tf_op jit(solution)/shard_map/ppermute | solution.py:541
  123.5 2.7 collective-permute-start.24
  126.1 15.0 %qkv.3 = (bf16[2048,512]{1,0:T(8,128)(2,1)}, bf16[4096,256]{1,0:T(8,128)(2,1)}, bf16[4096,256]{1,0:T(8,128)(2,1)}, bf16[2048,256]{1,0:T(8,128)(2,1)}) custom-call(bf16[2048,2048]{1,0:T(8,128)(2,1)} %ln.3.refs_0_, f32[2048,128]{1,0:T(8,128)} %get-tuple-element.122.refs_1_, ...), custom_call_target="tpu_custom_call", output_to_operand_aliasing={{1}: (14, {}), {2}: (15, {})} | custom-call | flops 8589934592 | bytes 16777216 | tf_op jit(solution)/shard_map/qkv/pallas_call | solution.py:120
  141.1 15.1 %attn.3.refs_33_ = bf16[2048,4608]{1,0:T(8,128)(2,1)} custom-call(bf16[2048,512]{1,0:T(8,128)(2,1)} %get-tuple-element.81.q_ref, bf16[4096,256]{1,0:T(8,128)(2,1)} %get-tuple-element.82.k_ref, bf16[2048,256]{1,0:T(8,128)(2,1)} %get-tuple-element.83.v_ref, s32[2,1,2048]{2,1,0:T(1,128)} %reshape.36.valid_ref), custom_call_target="tpu_custom_call" | custom-call | flops 16000000000 | bytes 6291456 | tf_op jit(solution)/shard_map/attn/pallas_call | solution.py:179
  167.5 33.5 %gate_up.5.refs_33_ = bf16[2048,4608]{1,0:T(8,128)(2,1)} custom-call(bf16[2048,2048]{1,0:T(8,128)(2,1)} %ln.2.refs_0_, bf16[128,5120]{1,0:T(8,128)(2,1)} %copy-done.1, bf16[128,5120]{1,0:T(8,128)(2,1)} %copy-done, bf16[128,5120]{1,0:T(8,128)(2,1)} %collective-permute-done.17.refs_3_.refs_19_, ...), custom_call_target="tpu_custom_call", output_to_operand_aliasing={{}: (33, {})} | custom-call | flops 25769803776 | bytes 16777216 | tf_op jit(solution)/shard_map/gate_up/pallas_call | solution.py:222
  204.1 17.2 %collective-permute-done.33.refs_13_.refs_29_ = bf16[128,3072]{1,0:T(8,128)(2,1)} collective-permute-done((bf16[128,3072]{1,0:T(8,128)(2,1)}, bf16[128,3072]{1,0:T(8,128)(2,1)}, u32[]{:S(2)}, u32[]{:S(2)}) %collective-permute-start.33) | collective-permute-done | bytes 786464 | tf_op jit(solution)/shard_map/ppermute | solution.py:541
  221.4 23.7 %gate_up.6.refs_33_ = bf16[2048,4608]{1,0:T(8,128)(2,1)} custom-call(bf16[2048,2048]{1,0:T(8,128)(2,1)} %ln.2.refs_0_, bf16[128,5120]{1,0:T(8,128)(2,1)} %copy-done.1, bf16[128,5120]{1,0:T(8,128)(2,1)} %copy-done, bf16[128,5120]{1,0:T(8,128)(2,1)} %collective-permute-done.17.refs_3_.refs_19_, ...), custom_call_target="tpu_custom_call", output_to_operand_aliasing={{}: (33, {})} | custom-call | flops 17179869184 | bytes 16777216 | tf_op jit(solution)/shard_map/gate_up/pallas_call | solution.py:222
  247.5 2.6 collective-permute-done.29.refs_7_.refs_23_
  257.7 33.5 %gate_up.7.act_ref = bf16[2048,4608]{1,0:T(8,128)(2,1)} custom-call(bf16[2048,2048]{1,0:T(8,128)(2,1)} %ln.2.refs_0_, bf16[128,3072]{1,0:T(8,128)(2,1)} %pad_maximum_fusion.3.refs_1_.refs_17_, bf16[128,3072]{1,0:T(8,128)(2,1)} %pad_maximum_fusion.4.refs_2_.refs_18_, bf16[128,3072]{1,0:T(8,128)(2,1)} %copy-done.16, ...), custom_call_target="tpu_custom_call", output_to_operand_aliasing={{}: (33, {})} | custom-call | flops 25769803776 | bytes 16777216 | tf_op jit(solution)/shard_map/gate_up/pallas_call | solution.py:222
  291.3 16.6 %down.3 = bf16[2048,512]{1,0:T(8,128)(2,1)} custom-call(bf16[2048,4608]{1,0:T(8,128)(2,1)} %gate_up.7.act_ref, bf16[2304,256]{1,0:T(8,128)(2,1)} %copy-done.10, bf16[2304,256]{1,0:T(8,128)(2,1)} %copy-done.9, bf16[2304,256]{1,0:T(8,128)(2,1)} %copy-done.14, bf16[2304,256]{1,0:T(8,128)(2,1)} %collective-permute-done.38.refs_3_.refs_5_), custom_call_target="tpu_custom_call" | custom-call | flops 9663676416 | bytes 18874368 | tf_op jit(solution)/shard_map/down/pallas_call | solution.py:287
  316.3 27.2 %down.4.refs_4_ = bf16[2048,1536]{1,0:T(8,128)(2,1)} custom-call(bf16[2048,4608]{1,0:T(8,128)(2,1)} %gate_up.7.act_ref, bf16[2304,256]{1,0:T(8,128)(2,1)} %collective-permute-done.39.refs_0_.refs_6_, bf16[2304,256]{1,0:T(8,128)(2,1)} %collective-permute-done.41.refs_1_.refs_7_, bf16[2304,256]{1,0:T(8,128)(2,1)} %collective-permute-done.45.refs_2_.refs_8_, ...), custom_call_target="tpu_custom_call" | custom-call | flops 19327352832 | bytes 18874368 | tf_op jit(solution)/shard_map/down/pallas_call | solution.py:287
  348.3 16.7 %down.5 = bf16[2048,1536]{1,0:T(8,128)(2,1)} custom-call(bf16[2048,4608]{1,0:T(8,128)(2,1)} %gate_up.7.act_ref, bf16[2304,256]{1,0:T(8,128)(2,1)} %copy-done.5, bf16[2304,256]{1,0:T(8,128)(2,1)} %copy-done.6, bf16[2304,256]{1,0:T(8,128)(2,1)} %copy-done.7, ...), custom_call_target="tpu_custom_call", output_to_operand_aliasing={{}: (5, {})} | custom-call | flops 9663676416 | bytes 18874368 | tf_op jit(solution)/shard_map/down/pallas_call | solution.py:287
  365.2 53.0 %gate_up.8.refs_33_ = bf16[2048,4608]{1,0:T(8,128)(2,1)} custom-call(bf16[2048,2048]{1,0:T(8,128)(2,1)} %ln.3.refs_0_, bf16[128,5120]{1,0:T(8,128)(2,1)} %copy-done.1, bf16[128,5120]{1,0:T(8,128)(2,1)} %copy-done, bf16[128,5120]{1,0:T(8,128)(2,1)} %collective-permute-done.17.refs_3_.refs_19_, ...), custom_call_target="tpu_custom_call", output_to_operand_aliasing={{}: (33, {})} | custom-call | flops 42949672960 | bytes 16777216 | tf_op jit(solution)/shard_map/gate_up/pallas_call | solution.py:222
  418.1 33.6 %gate_up.9.refs_0_ = bf16[2048,4608]{1,0:T(8,128)(2,1)} custom-call(bf16[2048,2048]{1,0:T(8,128)(2,1)} %ln.3.refs_0_, bf16[128,3072]{1,0:T(8,128)(2,1)} %pad_maximum_fusion.3.refs_1_.refs_17_, bf16[128,3072]{1,0:T(8,128)(2,1)} %pad_maximum_fusion.4.refs_2_.refs_18_, bf16[128,3072]{1,0:T(8,128)(2,1)} %copy-done.16, ...), custom_call_target="tpu_custom_call", output_to_operand_aliasing={{}: (33, {})} | custom-call | flops 25769803776 | bytes 16777216 | tf_op jit(solution)/shard_map/gate_up/pallas_call | solution.py:222
  451.8 176.2 %down_ring.1.refs_2_ = bf16[2048,2048]{1,0:T(8,128)(2,1)} custom-call(bf16[2048,4608]{1,0:T(8,128)(2,1)} %gate_up.9.refs_0_, bf16[4096,2048]{1,0:T(8,128)(2,1)} %bitcast.19, bf16[2304,256]{1,0:T(8,128)(2,1)} %copy-done.10, bf16[2304,256]{1,0:T(8,128)(2,1)} %copy-done.9, bf16[2304,256]{1,0:T(8,128)(2,1)} %copy-done.14, ...), custom_call_target="tpu_custom_call" | custom-call | flops 140000002048 | bytes 18874368 | tf_op jit(solution)/shard_map/down_ring/pallas_call | solution.py:465
  628.0 17.4 %residual.1 = bf16[4096,2048]{1,0:T(8,128)(2,1)} custom-call(s32[8]{0:T(128)} %stack.35.idx_ref, bf16[4096,2048]{1,0:T(8,128)(2,1)} %bitcast.20, bf16[2048,512]{1,0:T(8,128)(2,1)} %all-reduce.3.cloned.1.call-done.refs_0_, bf16[2048,1536]{1,0:T(8,128)(2,1)} %all-reduce.5.cloned.1.call-done.refs_1_, bf16[2048,2048]{1,0:T(8,128)(2,1)} %down_ring.1.refs_2_), custom_call_target="tpu_custom_call" | custom-call | flops 5000000000 | bytes 50331648 | tf_op jit(solution)/shard_map/residual/pallas_call | solution.py:506
  (164 shorter events, 59.3 us)
Async XLA Ops:
  7.2 357.9 %all-reduce.3.cloned.1.call-start = ((), (), s32[]{:S(2)}) async-start(), calls=%async_computation | async-start | bytes 4194304 | tf_op jit(solution)/shard_map/psum | solution.py:651
  9.2 50.1 %collective-permute-start.8 = (bf16[256,1024]{1,0:T(8,128)(2,1)S(1)}, bf16[256,1024]{1,0:T(8,128)(2,1)}, u32[]{:S(2)}, u32[]{:S(2)}) collective-permute-start(bf16[256,1024]{1,0:T(8,128)(2,1)S(1)} %constant_dynamic-update-slice_fusion.refs_4_), channel_id=1, source_target_pairs={{0,1},{1,0},{2,3},{3,2},{4,5},{5,4},{6,7},{7,6},{8,9},{9,8},{10,11... | collective-permute-start | bytes 1572872 | tf_op jit(solution)/shard_map/ppermute | solution.py:541
  59.4 35.6 %collective-permute-start.7 = (bf16[128,5120]{1,0:T(8,128)(2,1)S(1)}, bf16[128,5120]{1,0:T(8,128)(2,1)}, u32[]{:S(2)}, u32[]{:S(2)}) collective-permute-start(bf16[128,5120]{1,0:T(8,128)(2,1)S(1)} %pad_maximum_fusion.refs_1_.refs_17_), channel_id=1, source_target_pairs={{0,6},{1,7},{2,0},{3,1},{4,2},{5,3},{6,4},{7,5},{8,14},{9,15},{10,... | collective-permute-start | bytes 3932168 | tf_op jit(solution)/shard_map/ppermute | solution.py:541
  62.3 59.1 %collective-permute-start.6 = (bf16[128,5120]{1,0:T(8,128)(2,1)S(1)}, bf16[128,5120]{1,0:T(8,128)(2,1)}, u32[]{:S(2)}, u32[]{:S(2)}) collective-permute-start(bf16[128,5120]{1,0:T(8,128)(2,1)S(1)} %pad_maximum_fusion.1.refs_2_.refs_18_), channel_id=1, source_target_pairs={{0,2},{1,3},{2,4},{3,5},{4,6},{5,7},{6,0},{7,1},{8,10},{9,11},{10,... | collective-permute-start | bytes 3932168 | tf_op jit(solution)/shard_map/ppermute | solution.py:541
  62.5 58.9 %collective-permute-start.5 = (bf16[128,5120]{1,0:T(8,128)(2,1)S(1)}, bf16[128,5120]{1,0:T(8,128)(2,1)}, u32[]{:S(2)}, u32[]{:S(2)}) collective-permute-start(bf16[128,5120]{1,0:T(8,128)(2,1)S(1)} %pad_maximum_fusion.1.refs_2_.refs_18_), channel_id=1, source_target_pairs={{0,6},{1,7},{2,0},{3,1},{4,2},{5,3},{6,4},{7,5},{8,14},{9,15},{10,... | collective-permute-start | bytes 3932168 | tf_op jit(solution)/shard_map/ppermute | solution.py:541
  121.4 35.7 %collective-permute-start.17 = (bf16[128,5120]{1,0:T(8,128)(2,1)S(1)}, bf16[128,5120]{1,0:T(8,128)(2,1)}, u32[]{:S(2)}, u32[]{:S(2)}) collective-permute-start(bf16[128,5120]{1,0:T(8,128)(2,1)S(1)} %pad_maximum_fusion.refs_1_.refs_17_), channel_id=1, source_target_pairs={{0,1},{1,0},{2,3},{3,2},{4,5},{5,4},{6,7},{7,6},{8,9},{9,8},{10,11... | collective-permute-start | bytes 3932168 | tf_op jit(solution)/shard_map/ppermute | solution.py:541
  122.9 34.5 %collective-permute-start.18 = (bf16[128,5120]{1,0:T(8,128)(2,1)S(1)}, bf16[128,5120]{1,0:T(8,128)(2,1)}, u32[]{:S(2)}, u32[]{:S(2)}) collective-permute-start(bf16[128,5120]{1,0:T(8,128)(2,1)S(1)} %pad_maximum_fusion.1.refs_2_.refs_18_), channel_id=1, source_target_pairs={{0,1},{1,0},{2,3},{3,2},{4,5},{5,4},{6,7},{7,6},{8,9},{9,8},{10,11... | collective-permute-start | bytes 3932168 | tf_op jit(solution)/shard_map/ppermute | solution.py:541
  123.1 34.6 %collective-permute-start.20 = (bf16[128,5120]{1,0:T(8,128)(2,1)}, bf16[128,5120]{1,0:T(8,128)(2,1)}, u32[]{:S(2)}, u32[]{:S(2)}) collective-permute-start(bf16[128,5120]{1,0:T(8,128)(2,1)} %collective-permute-done.6.refs_6_.refs_22_), channel_id=1, source_target_pairs={{0,1},{1,0},{2,3},{3,2},{4,5},{5,4},{6,7},{7,6},{8,9},{9,8},{10,11... | collective-permute-start | bytes 3932168 | tf_op jit(solution)/shard_map/ppermute | solution.py:541
  123.5 33.5 %collective-permute-start.24 = (bf16[128,5120]{1,0:T(8,128)(2,1)}, bf16[128,5120]{1,0:T(8,128)(2,1)}, u32[]{:S(2)}, u32[]{:S(2)}) collective-permute-start(bf16[128,5120]{1,0:T(8,128)(2,1)} %collective-permute-done.5.refs_10_.refs_26_), channel_id=1, source_target_pairs={{0,6},{1,7},{2,0},{3,1},{4,2},{5,3},{6,4},{7,5},{8,14},{9,15},{10,... | collective-permute-start | bytes 3932168 | tf_op jit(solution)/shard_map/ppermute | solution.py:541
  160.0 41.0 %collective-permute-start.16 = (bf16[128,3072]{1,0:T(8,128)(2,1)}, bf16[128,3072]{1,0:T(8,128)(2,1)}, u32[]{:S(2)}, u32[]{:S(2)}) collective-permute-start(bf16[128,3072]{1,0:T(8,128)(2,1)} %pad_maximum_fusion.3.refs_1_.refs_17_), channel_id=1, source_target_pairs={{0,6},{1,7},{2,0},{3,1},{4,2},{5,3},{6,4},{7,5},{8,14},{9,15},{10,... | collective-permute-start | bytes 2359304 | tf_op jit(solution)/shard_map/ppermute | solution.py:541
  161.8 39.1 %collective-permute-start.13 = (bf16[128,3072]{1,0:T(8,128)(2,1)}, bf16[128,3072]{1,0:T(8,128)(2,1)}, u32[]{:S(2)}, u32[]{:S(2)}) collective-permute-start(bf16[128,3072]{1,0:T(8,128)(2,1)} %pad_maximum_fusion.3.refs_1_.refs_17_), channel_id=1, source_target_pairs={{0,2},{1,3},{2,4},{3,5},{4,6},{5,7},{6,0},{7,1},{8,10},{9,11},{10,... | collective-permute-start | bytes 2359304 | tf_op jit(solution)/shard_map/ppermute | solution.py:541
  163.6 37.4 %collective-permute-start.15 = (bf16[128,3072]{1,0:T(8,128)(2,1)S(1)}, bf16[128,3072]{1,0:T(8,128)(2,1)}, u32[]{:S(2)}, u32[]{:S(2)}) collective-permute-start(bf16[128,3072]{1,0:T(8,128)(2,1)S(1)} %copy-done.11), channel_id=1, source_target_pairs={{0,2},{1,3},{2,4},{3,5},{4,6},{5,7},{6,0},{7,1},{8,10},{9,11},{10,... | collective-permute-start | bytes 2359304 | tf_op jit(solution)/shard_map/ppermute | solution.py:541
  165.5 35.5 %collective-permute-start.14 = (bf16[128,3072]{1,0:T(8,128)(2,1)S(1)}, bf16[128,3072]{1,0:T(8,128)(2,1)}, u32[]{:S(2)}, u32[]{:S(2)}) collective-permute-start(bf16[128,3072]{1,0:T(8,128)(2,1)S(1)} %copy-done.11), channel_id=1, source_target_pairs={{0,6},{1,7},{2,0},{3,1},{4,2},{5,3},{6,4},{7,5},{8,14},{9,15},{10,... | collective-permute-start | bytes 2359304 | tf_op jit(solution)/shard_map/ppermute | solution.py:541
  202.8 43.6 %collective-permute-start.27 = (bf16[128,3072]{1,0:T(8,128)(2,1)}, bf16[128,3072]{1,0:T(8,128)(2,1)S(1)}, u32[]{:S(2)}, u32[]{:S(2)}) collective-permute-start(bf16[128,3072]{1,0:T(8,128)(2,1)} %pad_maximum_fusion.3.refs_1_.refs_17_), channel_id=1, source_target_pairs={{0,1},{1,0},{2,3},{3,2},{4,5},{5,4},{6,7},{7,6},{8,9},{9,8},{10,11... | collective-permute-start | bytes 2359304 | tf_op jit(solution)/shard_map/ppermute | solution.py:541
  203.5 43.1 %collective-permute-start.28 = (bf16[128,3072]{1,0:T(8,128)(2,1)S(1)}, bf16[128,3072]{1,0:T(8,128)(2,1)}, u32[]{:S(2)}, u32[]{:S(2)}) collective-permute-start(bf16[128,3072]{1,0:T(8,128)(2,1)S(1)} %copy-done.11), channel_id=1, source_target_pairs={{0,1},{1,0},{2,3},{3,2},{4,5},{5,4},{6,7},{7,6},{8,9},{9,8},{10,11... | collective-permute-start | bytes 2359304 | tf_op jit(solution)/shard_map/ppermute | solution.py:541
  203.6 43.3 %collective-permute-start.30 = (bf16[128,3072]{1,0:T(8,128)(2,1)}, bf16[128,3072]{1,0:T(8,128)(2,1)}, u32[]{:S(2)}, u32[]{:S(2)}) collective-permute-start(bf16[128,3072]{1,0:T(8,128)(2,1)} %collective-permute-done.15.refs_6_.refs_22_), channel_id=1, source_target_pairs={{0,1},{1,0},{2,3},{3,2},{4,5},{5,4},{6,7},{7,6},{8,9},{9,8},{10,11... | collective-permute-start | bytes 2359304 | tf_op jit(solution)/shard_map/ppermute | solution.py:541
  204.0 43.1 %collective-permute-start.31 = (bf16[128,3072]{1,0:T(8,128)(2,1)}, bf16[128,3072]{1,0:T(8,128)(2,1)}, u32[]{:S(2)}, u32[]{:S(2)}) collective-permute-start(bf16[128,3072]{1,0:T(8,128)(2,1)} %collective-permute-done.16.refs_9_.refs_25_), channel_id=1, source_target_pairs={{0,1},{1,0},{2,3},{3,2},{4,5},{5,4},{6,7},{7,6},{8,9},{9,8},{10,11... | collective-permute-start | bytes 2359304 | tf_op jit(solution)/shard_map/ppermute | solution.py:541
  250.0 57.9 %collective-permute-start.42 = (bf16[2304,256]{1,0:T(8,128)(2,1)S(1)}, bf16[2304,256]{1,0:T(8,128)(2,1)}, u32[]{:S(2)}, u32[]{:S(2)}) collective-permute-start(bf16[2304,256]{1,0:T(8,128)(2,1)S(1)} %get-tuple-element.97.refs_0_.refs_2_), channel_id=1, source_target_pairs={{0,6},{1,7},{2,0},{3,1},{4,2},{5,3},{6,4},{7,5},{8,14},{9,15},{10,... | collective-permute-start | bytes 3538952 | tf_op jit(solution)/shard_map/ppermute | solution.py:541
  251.1 56.8 %collective-permute-start.39 = (bf16[2304,256]{1,0:T(8,128)(2,1)S(1)}, bf16[2304,256]{1,0:T(8,128)(2,1)}, u32[]{:S(2)}, u32[]{:S(2)}) collective-permute-start(bf16[2304,256]{1,0:T(8,128)(2,1)S(1)} %get-tuple-element.97.refs_0_.refs_2_), channel_id=1, source_target_pairs={{0,2},{1,3},{2,4},{3,5},{4,6},{5,7},{6,0},{7,1},{8,10},{9,11},{10,... | collective-permute-start | bytes 3538952 | tf_op jit(solution)/shard_map/ppermute | solution.py:541
  252.9 55.0 %collective-permute-start.41 = (bf16[2304,256]{1,0:T(8,128)(2,1)S(1)}, bf16[2304,256]{1,0:T(8,128)(2,1)}, u32[]{:S(2)}, u32[]{:S(2)}) collective-permute-start(bf16[2304,256]{1,0:T(8,128)(2,1)S(1)} %get-tuple-element.98.refs_1_.refs_3_), channel_id=1, source_target_pairs={{0,2},{1,3},{2,4},{3,5},{4,6},{5,7},{6,0},{7,1},{8,10},{9,11},{10,... | collective-permute-start | bytes 3538952 | tf_op jit(solution)/shard_map/ppermute | solution.py:541
  253.3 54.6 %collective-permute-start.40 = (bf16[2304,256]{1,0:T(8,128)(2,1)S(1)}, bf16[2304,256]{1,0:T(8,128)(2,1)}, u32[]{:S(2)}, u32[]{:S(2)}) collective-permute-start(bf16[2304,256]{1,0:T(8,128)(2,1)S(1)} %get-tuple-element.98.refs_1_.refs_3_), channel_id=1, source_target_pairs={{0,6},{1,7},{2,0},{3,1},{4,2},{5,3},{6,4},{7,5},{8,14},{9,15},{10,... | collective-permute-start | bytes 3538952 | tf_op jit(solution)/shard_map/ppermute | solution.py:541
  256.5 34.8 %collective-permute-start.38 = (bf16[2304,256]{1,0:T(8,128)(2,1)S(1)}, bf16[2304,256]{1,0:T(8,128)(2,1)}, u32[]{:S(2)}, u32[]{:S(2)}) collective-permute-start(bf16[2304,256]{1,0:T(8,128)(2,1)S(1)} %get-tuple-element.98.refs_1_.refs_3_), channel_id=1, source_target_pairs={{0,1},{1,0},{2,3},{3,2},{4,5},{5,4},{6,7},{7,6},{8,9},{9,8},{10,11... | collective-permute-start | bytes 3538952 | tf_op jit(solution)/shard_map/ppermute | solution.py:541
  309.1 318.9 %all-reduce.5.cloned.1.call-start = ((), (), s32[]{:S(2)}) async-start(), calls=%async_computation.1 | async-start | bytes 12582912 | tf_op jit(solution)/shard_map/psum | solution.py:661
  309.2 34.3 %collective-permute-start.43 = (bf16[2304,256]{1,0:T(8,128)(2,1)}, bf16[2304,256]{1,0:T(8,128)(2,1)S(1)}, u32[]{:S(2)}, u32[]{:S(2)}) collective-permute-start(bf16[2304,256]{1,0:T(8,128)(2,1)} %collective-permute-done.39.refs_0_.refs_6_), channel_id=1, source_target_pairs={{0,2},{1,3},{2,4},{3,5},{4,6},{5,7},{6,0},{7,1},{8,10},{9,11},{10,... | collective-permute-start | bytes 3538952 | tf_op jit(solution)/shard_map/ppermute | solution.py:541
  (52 other events, 868.2 us)
Sparse Core Ops, SparseCore 0:
  309.2 53.6 all-reduce.2
  365.9 127.8 all-reduce.4
